TPU v7x, 32 devices: a whole 2x2x4 slice. The times are simulated.
32 devices in a mesh: dp: 8 (over z, core), row: 2 (over x), col: 2 (over y).
Axes of the slice: x: 2, y: 2, z: 4, core: 2. Of those that a mesh axis runs over, the one named last changes fastest.
Arguments:
- tokens: bfloat16 [4096, 8192], P(('dp', 'row', 'col')), parts along dimension 0, may hold values from -6 to 6
- w_gate: bfloat16 [8192, 1024], P(('row', 'col')), may hold values from -0.0625 to 0.0625
- w_up: bfloat16 [8192, 1024], P(('row', 'col')), may hold values from -0.0625 to 0.0625
- w_down: bfloat16 [1024, 8192], P(None, ('row', 'col')), may hold values from -0.1875 to 0.1875
Outputs:
- mixed: bfloat16 [4096, 8192], P(('dp', 'row', 'col')), parts along dimension 0
There are 8 independent parts, one for each index of `dp`. A program takes and returns all parts, laid end to end along the dimension named above; an argument that names none is the same for every part. Nothing has to cross between parts.
All inputs are finite; a program needn't handle non-finite values.
Results may differ from a plain program's by a relative error of at most 0.029.
Values may be sent and summed in bfloat16 or wider, within the bound.
A program may use at most 64 MiB of HBM per device.

v0:
```python
import functools

import jax
import jax.numpy as jnp
from jax import lax
from jax.experimental import pallas as pl
from jax.experimental.pallas import tpu as pltpu
from jax.sharding import PartitionSpec as P

MESH = pl.DeviceIdType.MESH
CHUNKS = 4
AHEAD = 3
EARLY_HOPS = 2


def tile_of(width, most):
    tile = min(width, most)
    while width % tile:
        tile //= 2
    return tile


def kernel(
    groups, rows, cols, chunks,
    x_ref, wg_ref, wu_ref, wd_ref, out_ref,
    wg, wu, wa, wb, xbuf, acc, part, rec_a, rec_b, sum_a, sum_b, fin_a, fin_b, ha, hb, oa, ob,
    w_sem, fa_sem, fb_sem, up_sem, down_sem, land_sem, mate_sem,
    x_sem, a_sem, b_sem, c_sem, d_sem, ha_sem, hb_sem, oa_sem, ob_sem,
):
    n = rows * cols
    row, col = lax.axis_index("row"), lax.axis_index("col")
    group = lax.axis_index("dp")
    mates = 2 - groups % 2
    planes = groups // mates
    plane, core = group // mates, lax.rem(group, mates)
    t = x_ref.shape[0] // chunks
    features, hidden = wg.shape
    half = hidden // 2
    side_cols = wa.shape[2]
    share = hidden // groups
    bf16, f32 = jnp.bfloat16, jnp.float32

    def up(r, c):
        return lax.rem(row + r, rows), lax.rem(col + c, cols)

    def down(r, c):
        return lax.rem(row + rows - r, rows), lax.rem(col + cols - c, cols)

    def shard(rc, width):
        return pl.ds(pl.multiple_of((rc[0] * cols + rc[1]) * width, width), width)

    def remote(src, dst, sems, index, to):
        return pltpu.make_async_remote_copy(
            src_ref=src, dst_ref=dst,
            send_sem=sems.at[(0, *index)], recv_sem=sems.at[(1, *index)],
            device_id={"row": to[0], "col": to[1]}, device_id_type=MESH,
        )

    def tok(k):
        return pl.ds(pl.multiple_of(k * t, t), t)

    slots = [(r, c) for r in range(rows) for c in range(cols)]
    others = slots[1:]
    by_reach = others[::-1]

    def at_slot(r, c):
        return pl.ds((r * cols + c) * t, t)

    def x_copy(k, r, c):
        to = up(r, c)
        return remote(
            x_ref.at[tok(k), shard(to, features)], xbuf.at[k, at_slot(r, c)],
            x_sem, (k, r * cols + c), to,
        )

    def x_own(k):
        return pltpu.make_async_copy(
            x_ref.at[tok(k), shard((row, col), features)], xbuf.at[k, at_slot(0, 0)], x_sem.at[1, k, 0]
        )

    def a_copy(k, r):
        return remote(part.at[k, 0, r], rec_a.at[k, r], a_sem, (k, r), down(r, 0))

    def b_copy(k, c):
        return remote(part.at[k, 1, :, c], rec_b.at[k, c], b_sem, (k, c), down(0, c))

    def c_copy(k, c):
        return remote(sum_a.at[k, c], fin_a.at[k, c], c_sem, (k, c), down(0, c))

    def d_copy(k, r):
        return remote(sum_b.at[k, r], fin_b.at[k, r], d_sem, (k, r), down(r, 0))

    def share_of(g):
        return pl.ds(pl.multiple_of(g * share, share), share)

    def fetch_a(c):
        return remote(
            wd_ref.at[share_of(group), pl.ds(0, side_cols)], wa.at[c, share_of(group)],
            fa_sem, (c,), down(0, c),
        )

    def fetch_b(r):
        return remote(
            wd_ref.at[share_of(group), pl.ds(side_cols, side_cols)], wb.at[r, share_of(group)],
            fb_sem, (r,), down(r, 0),
        )

    blocks = [(wa, c, c) for c in range(1, cols)] + [(wb, r, cols + r) for r in range(1, rows)]

    def pass_on(source, block, sems, to_plane):
        ref, slot, index = block
        region = ref.at[slot, share_of(source * mates + core)]
        return pltpu.make_async_remote_copy(
            src_ref=region, dst_ref=region,
            send_sem=sems.at[source, index], recv_sem=land_sem.at[source, index],
            device_id={"dp": to_plane * mates + core}, device_id_type=MESH,
        )

    def to_mate(source, block, whose):
        ref, slot, index = block
        region = ref.at[slot, share_of(source * mates + whose)]
        return pltpu.make_async_remote_copy(
            src_ref=region, dst_ref=region,
            send_sem=mate_sem.at[0, source, index], recv_sem=mate_sem.at[1, source, index],
            device_id={"dp": plane * mates + (mates - 1 - core)}, device_id_type=MESH,
        )

    def spread(source, upward, downward):
        for block in blocks:
            if mates > 1:
                to_mate(source, block, core).start()
            if upward:

                @pl.when(plane + 1 < planes)
                def _():
                    pass_on(source, block, up_sem, plane + 1).start()

            if downward:

                @pl.when(plane > 0)
                def _():
                    pass_on(source, block, down_sem, plane - 1).start()

    def hop(h):
        below, above = plane - h, plane + h

        @pl.when(below >= 0)
        def _():
            for block in blocks:
                pass_on(below, block, up_sem, plane).wait_recv()
            spread(below, True, False)

        @pl.when(above < planes)
        def _():
            for block in blocks:
                pass_on(above, block, down_sem, plane).wait_recv()
            spread(above, False, True)

    def last_hops():
        def more(h, _):
            hop(h)
            return 0

        lax.fori_loop(EARLY_HOPS + 1, planes, more, 0)
        if mates > 1:

            def landed(z, _):
                for block in blocks:
                    to_mate(z, block, mates - 1 - core).wait_recv()
                return 0

            lax.fori_loop(0, planes, landed, 0)

    def sent(z, _):
        for block in blocks:
            if mates > 1:
                to_mate(z, block, core).wait_send()

            @pl.when(jnp.logical_and(plane + 1 < planes, z <= plane))
            def _():
                pass_on(z, block, up_sem, plane).wait_send()

            @pl.when(jnp.logical_and(plane > 0, z >= plane))
            def _():
                pass_on(z, block, down_sem, plane).wait_send()

        return 0

    def ha_copy(k, r):
        return remote(ha.at[k, pl.ds(0, t)], ha.at[k, pl.ds(r * t, t)], ha_sem, (k, r), up(r, 0))

    def hb_copy(k, c):
        return remote(hb.at[k, pl.ds(0, t)], hb.at[k, pl.ds(c * t, t)], hb_sem, (k, c), up(0, c))

    def out_at(k, rc, side):
        start = (rc[0] * cols + rc[1]) * 2 * side_cols + side * side_cols
        return out_ref.at[tok(k), pl.ds(pl.multiple_of(start, side_cols), side_cols)]

    def oa_copy(k, r, c, columns_of):
        return remote(
            oa.at[k, c, pl.ds(r * t, t)], out_at(k, columns_of, 0), oa_sem, (k, r, c), down(r, 0)
        )

    def ob_copy(k, r, c, columns_of):
        return remote(
            ob.at[k, r, pl.ds(c * t, t)], out_at(k, columns_of, 1), ob_sem, (k, r, c), down(0, c)
        )

    def oa_own(k, c):
        return pltpu.make_async_copy(
            oa.at[k, c, pl.ds(0, t)], out_at(k, up(0, c), 0), oa_sem.at[1, k, 0, c]
        )

    def ob_own(k, r):
        return pltpu.make_async_copy(
            ob.at[k, r, pl.ds(0, t)], out_at(k, up(r, 0), 1), ob_sem.at[1, k, r, 0]
        )

    loads = [
        pltpu.make_async_copy(wg_ref, wg, w_sem.at[0]),
        pltpu.make_async_copy(wu_ref, wu, w_sem.at[1]),
        pltpu.make_async_copy(wd_ref.at[:, pl.ds(0, side_cols)], wa.at[0], w_sem.at[2]),
        pltpu.make_async_copy(wd_ref.at[:, pl.ds(side_cols, side_cols)], wb.at[0], w_sem.at[3]),
    ]

    barrier = pltpu.get_barrier_semaphore()
    for r, c in others:
        to = up(r, c)
        pl.semaphore_signal(barrier, inc=1, device_id={"row": to[0], "col": to[1]}, device_id_type=MESH)
    def greet(g):
        pl.semaphore_signal(barrier, inc=1, device_id={"dp": g}, device_id_type=MESH)

    pl.when(plane > 0)(lambda: greet(group - mates))
    pl.when(plane + 1 < planes)(lambda: greet(group + mates))
    if mates > 1:
        greet(plane * mates + (mates - 1 - core))
    neighbours = (plane > 0).astype(jnp.int32) + (plane + 1 < planes).astype(jnp.int32)
    pl.semaphore_wait(barrier, n - 1 + mates - 1 + neighbours)

    for c in range(1, cols):
        fetch_a(c).start()
    for r in range(1, rows):
        fetch_b(r).start()

    def send_tokens(k):
        for r, c in by_reach:
            x_copy(k, r, c).start()

    for k in range(min(AHEAD, chunks)):
        send_tokens(k)
    for k in range(chunks):
        x_own(k).start()
    for load in loads:
        load.start()
    for c in range(1, cols):
        fetch_a(c).wait_recv()
    for r in range(1, rows):
        fetch_b(r).wait_recv()
    spread(plane, True, True)
    for load in loads:
        load.wait()

    tile = tile_of(half, 512)
    per_half = half // tile

    def project(k):
        x_own(k).wait()
        for r, c in others:
            x_copy(k, r, c).wait_recv()

        def column(j, _):
            side, at = j // per_half, lax.rem(j, per_half) * tile
            source = pl.ds(pl.multiple_of(j * tile, tile), tile)
            for w, base in ((wg, 0), (wu, half)):
                target = pl.ds(pl.multiple_of(base + at, tile), tile)
                got = jnp.dot(xbuf[k], w[:, source], preferred_element_type=f32)
                acc[k, side, :, target] = got[:t]
                for r, c in others:
                    first = (r * cols + c) * t
                    part[k, side, r, c, :, target] = got[first : first + t].astype(bf16)
            return 0

        lax.fori_loop(0, 2 * per_half, column, 0)
        for r in range(1, rows):
            a_copy(k, r).start()
        for c in range(1, cols):
            b_copy(k, c).start()

    def combine(k):
        for r in range(1, rows):
            a_copy(k, r).wait_recv()
        for c in range(1, cols):
            total = part[k, 0, 0, c].astype(f32)
            for r in range(1, rows):
                total = total + rec_a[k, r, c].astype(f32)
            sum_a[k, c] = total.astype(bf16)
            c_copy(k, c).start()
        for c in range(1, cols):
            b_copy(k, c).wait_recv()
        for r in range(1, rows):
            total = part[k, 1, r, 0].astype(f32)
            for c in range(1, cols):
                total = total + rec_b[k, c, r].astype(f32)
            sum_b[k, r] = total.astype(bf16)
            d_copy(k, r).start()

    def activate(k):
        for c in range(1, cols):
            c_copy(k, c).wait_recv()
        for r in range(1, rows):
            d_copy(k, r).wait_recv()
        for side in range(2):
            total = acc[k, side]
            if side == 0:
                for r in range(1, rows):
                    total = total + rec_a[k, r, 0].astype(f32)
                for c in range(1, cols):
                    total = total + fin_a[k, c].astype(f32)
            else:
                for c in range(1, cols):
                    total = total + rec_b[k, c, 0].astype(f32)
                for r in range(1, rows):
                    total = total + fin_b[k, r].astype(f32)
            gate = total[:, :half]
            done = (gate / (1.0 + jnp.exp(-gate)) * total[:, half:]).astype(bf16)
            ha[k, pl.ds(0, t), pl.ds(side * half, half)] = done
            hb[k, pl.ds(0, t), pl.ds(side * half, half)] = done
        for r in range(1, rows):
            ha_copy(k, r).start()
        for c in range(1, cols):
            hb_copy(k, c).start()

    out_tile = tile_of(side_cols, 512)
    out_tiles = side_cols // out_tile

    def emit(k):
        for r in range(1, rows):
            ha_copy(k, r).wait_recv()

        def columns_a(j, _):
            c = j // out_tiles
            where = pl.ds(pl.multiple_of(lax.rem(j, out_tiles) * out_tile, out_tile), out_tile)
            oa[k, c, :, where] = jnp.dot(
                ha[k], wa[c, :, where], preferred_element_type=f32
            ).astype(bf16)
            return 0

        lax.fori_loop(0, cols * out_tiles, columns_a, 0)
        for c in range(cols):
            for r in range(1, rows):
                oa_copy(k, r, c, up(0, c)).start()
        for c in range(1, cols):
            hb_copy(k, c).wait_recv()

        def columns_b(j, _):
            r = j // out_tiles
            where = pl.ds(pl.multiple_of(lax.rem(j, out_tiles) * out_tile, out_tile), out_tile)
            ob[k, r, :, where] = jnp.dot(
                hb[k], wb[r, :, where], preferred_element_type=f32
            ).astype(bf16)
            return 0

        lax.fori_loop(0, rows * out_tiles, columns_b, 0)
        for r in range(rows):
            for c in range(1, cols):
                ob_copy(k, r, c, up(r, 0)).start()
        for c in range(cols):
            oa_own(k, c).start()
        for r in range(rows):
            ob_own(k, r).start()

    stages = (project, combine, activate, emit)

    def step(s, _):
        for lag, stage in enumerate(stages):
            k = s - lag

            @pl.when(jnp.logical_and(k >= 0, k < chunks))
            def _():
                stage(k)

            if lag == 0:

                @pl.when(s + AHEAD < chunks)
                def _():
                    send_tokens(s + AHEAD)

                for h in range(1, min(EARLY_HOPS, planes - 1) + 1):
                    pl.when(s == h)(lambda h=h: hop(h))

                pl.when(s == len(stages) - 1)(last_hops)

        return 0

    lax.fori_loop(0, chunks + len(stages) - 1, step, 0)

    def finish(k, _):
        for r, c in others:
            x_copy(k, r, c).wait_send()
        for r, c in slots:
            if r:
                oa_copy(k, r, c, up(0, c)).wait_send()
                oa_copy(k, r, c, up(r, c)).wait_recv()
            else:
                oa_own(k, c).wait()
            if c:
                ob_copy(k, r, c, up(r, 0)).wait_send()
                ob_copy(k, r, c, up(r, c)).wait_recv()
            else:
                ob_own(k, r).wait()
        for r in range(1, rows):
            a_copy(k, r).wait_send()
            d_copy(k, r).wait_send()
            ha_copy(k, r).wait_send()
        for c in range(1, cols):
            b_copy(k, c).wait_send()
            c_copy(k, c).wait_send()
            hb_copy(k, c).wait_send()
        return 0

    lax.fori_loop(0, chunks, finish, 0)
    for c in range(1, cols):
        fetch_a(c).wait_send()
    for r in range(1, rows):
        fetch_b(r).wait_send()
    lax.fori_loop(0, planes, sent, 0)


def solution(mesh):
    groups, rows, cols = mesh.shape["dp"], mesh.shape["row"], mesh.shape["col"]
    planes = groups // (2 - groups % 2)
    n = rows * cols

    def shards(tokens, w_gate, w_up, w_down):
        count, width = tokens.shape
        features, hidden = w_gate.shape
        side_cols = w_down.shape[1] // 2
        chunks = CHUNKS
        t = count // chunks
        bf16 = jnp.bfloat16
        any_space = pl.BlockSpec(memory_space=pl.ANY)

        def sems(*shape):
            return pltpu.SemaphoreType.DMA((2, chunks, *shape))

        return pl.pallas_call(
            functools.partial(kernel, groups, rows, cols, chunks),
            out_shape=jax.ShapeDtypeStruct((count, width), bf16),
            in_specs=[any_space] * 4,
            out_specs=any_space,
            scratch_shapes=[
                pltpu.VMEM((features, hidden), bf16),
                pltpu.VMEM((features, hidden), bf16),
                pltpu.VMEM((cols, hidden, side_cols), bf16),
                pltpu.VMEM((rows, hidden, side_cols), bf16),
                pltpu.VMEM((chunks, n * t, features), bf16),
                pltpu.VMEM((chunks, 2, t, hidden), jnp.float32),
                pltpu.VMEM((chunks, 2, rows, cols, t, hidden), bf16),
                pltpu.VMEM((chunks, rows, cols, t, hidden), bf16),
                pltpu.VMEM((chunks, cols, rows, t, hidden), bf16),
                pltpu.VMEM((chunks, cols, t, hidden), bf16),
                pltpu.VMEM((chunks, rows, t, hidden), bf16),
                pltpu.VMEM((chunks, cols, t, hidden), bf16),
                pltpu.VMEM((chunks, rows, t, hidden), bf16),
                pltpu.VMEM((chunks, rows * t, hidden), bf16),
                pltpu.VMEM((chunks, cols * t, hidden), bf16),
                pltpu.VMEM((chunks, cols, rows * t, side_cols), bf16),
                pltpu.VMEM((chunks, rows, cols * t, side_cols), bf16),
                pltpu.SemaphoreType.DMA((4,)),
                pltpu.SemaphoreType.DMA((2, cols)),
                pltpu.SemaphoreType.DMA((2, rows)),
                pltpu.SemaphoreType.DMA((planes, cols + rows)),
                pltpu.SemaphoreType.DMA((planes, cols + rows)),
                pltpu.SemaphoreType.DMA((planes, cols + rows)),
                pltpu.SemaphoreType.DMA((2, planes, cols + rows)),
                sems(n), sems(rows), sems(cols), sems(cols), sems(rows),
                sems(rows), sems(cols), sems(rows, cols), sems(rows, cols),
            ],
            compiler_params=pltpu.CompilerParams(collective_id=0, has_side_effects=True),
        )(tokens, w_gate, w_up, w_down)

    in_specs = (
        P(("dp", "row", "col"), None),
        P(("row", "col"), None),
        P(("row", "col"), None),
        P(None, ("row", "col")),
    )
    out_specs = P(("dp", "row", "col"), None)
    return jax.shard_map(shards, mesh=mesh, in_specs=in_specs, out_specs=out_specs, check_vma=False)
```

profile of v0, /device:TPU:0, one launch (start us, length us, event | category | flops | bytes accessed | tf_op | source)
XLA Modules:
  0.0 73.7 jit_solution(14746550104305296161)
XLA Ops:
  0.0 70.6 %shard_map.46 = bf16[128,8192]{1,0:T(8,128)(2,1)} custom-call(bf16[128,8192]{1,0:T(8,128)(2,1)} %x_ref.1, bf16[2048,1024]{1,0:T(8,128)(2,1)} %wg_ref.1, bf16[2048,1024]{1,0:T(8,128)(2,1)} %wu_ref.1, bf16[1024,2048]{1,0:T(8,128)(2,1)} %wd_ref.1), custom_call_target="tpu_custom_call" | custom-call | tf_op jit(solution)/shard_map/pallas_call | solution.py:446
  70.6 3.1 %copy.6 = bf16[128,8192]{1,0:T(8,128)(2,1)} copy(bf16[128,8192]{1,0:T(8,128)(2,1)} %shard_map.46) | data formatting | bytes 4194304
where the time goes:
time: 75.1 us; the launch traced here: 73.7 us
  Pallas kernels  70.6 us (94%)
  local copies, waits for them, and re-layouts  3.1 us (4%)
    pallas_call x1, Pallas kernels, shards(): pl.pallas_call(functools.partial(kernel, groups, rows, cols, chunks), out...  70.6 us
    unnamed x1, local copies, waits for them, and re-layouts  3.1 us

commit v1 on v0

--- a/solution.py
+++ b/solution.py
@@ -9,8 +9,12 @@
 
 MESH = pl.DeviceIdType.MESH
 CHUNKS = 4
-AHEAD = 3
 EARLY_HOPS = 2
+ORDER = (
+    "fetch", "project 0", "project 1", "hop 1", "project 2", "project 3", "hop 2", "combine 0", "combine 1",
+    "last hops", "combine 2", "activate 0", "combine 3", "activate 1", "activate 2", "activate 3",
+    "emit 0", "emit 1", "local", "emit 2", "emit 3", "landed", "emit fetched",
+)
 
 
 def tile_of(width, most):
@@ -25,7 +29,7 @@
     x_ref, wg_ref, wu_ref, wd_ref, out_ref,
     wg, wu, wa, wb, xbuf, acc, part, rec_a, rec_b, sum_a, sum_b, fin_a, fin_b, ha, hb, oa, ob,
     w_sem, fa_sem, fb_sem, up_sem, down_sem, land_sem, mate_sem,
-    x_sem, a_sem, b_sem, c_sem, d_sem, ha_sem, hb_sem, oa_sem, ob_sem,
+    x_sem, a_sem, b_sem, c_sem, d_sem, ha_sem, hb_sem, oa_sem, ob_sem, ga_sem, gb_sem,
 ):
     n = rows * cols
     row, col = lax.axis_index("row"), lax.axis_index("col")
@@ -105,7 +109,9 @@
             fb_sem, (r,), down(r, 0),
         )
 
-    blocks = [(wa, c, c) for c in range(1, cols)] + [(wb, r, cols + r) for r in range(1, rows)]
+    blocks_a = [(wa, c, c) for c in range(1, cols)]
+    blocks_b = [(wb, r, cols + r) for r in range(1, rows)]
+    blocks = blocks_a + blocks_b
 
     def pass_on(source, block, sems, to_plane):
         ref, slot, index = block
@@ -125,10 +131,8 @@
             device_id={"dp": plane * mates + (mates - 1 - core)}, device_id_type=MESH,
         )
 
-    def spread(source, upward, downward):
-        for block in blocks:
-            if mates > 1:
-                to_mate(source, block, core).start()
+    def spread(source, some, upward, downward):
+        for block in some:
             if upward:
 
                 @pl.when(plane + 1 < planes)
@@ -141,35 +145,41 @@
                 def _():
                     pass_on(source, block, down_sem, plane - 1).start()
 
-    def hop(h):
+            if mates > 1:
+                to_mate(source, block, core).start()
+
+    def hop(h, some):
         below, above = plane - h, plane + h
 
         @pl.when(below >= 0)
         def _():
-            for block in blocks:
+            for block in some:
                 pass_on(below, block, up_sem, plane).wait_recv()
-            spread(below, True, False)
+            spread(below, some, True, False)
 
         @pl.when(above < planes)
         def _():
-            for block in blocks:
+            for block in some:
                 pass_on(above, block, down_sem, plane).wait_recv()
-            spread(above, False, True)
+            spread(above, some, False, True)
 
     def last_hops():
         def more(h, _):
-            hop(h)
+            hop(h, blocks_a)
+            hop(h, blocks_b)
             return 0
 
         lax.fori_loop(EARLY_HOPS + 1, planes, more, 0)
+
+    def landed():
         if mates > 1:
 
-            def landed(z, _):
+            def from_mate(z, _):
                 for block in blocks:
                     to_mate(z, block, mates - 1 - core).wait_recv()
                 return 0
 
-            lax.fori_loop(0, planes, landed, 0)
+            lax.fori_loop(0, planes, from_mate, 0)
 
     def sent(z, _):
         for block in blocks:
@@ -187,33 +197,42 @@
         return 0
 
     def ha_copy(k, r):
-        return remote(ha.at[k, pl.ds(0, t)], ha.at[k, pl.ds(r * t, t)], ha_sem, (k, r), up(r, 0))
+        return remote(ha.at[0, tok(k)], ha.at[r, tok(k)], ha_sem, (k, r), up(r, 0))
 
     def hb_copy(k, c):
-        return remote(hb.at[k, pl.ds(0, t)], hb.at[k, pl.ds(c * t, t)], hb_sem, (k, c), up(0, c))
-
-    def out_at(k, rc, side):
-        start = (rc[0] * cols + rc[1]) * 2 * side_cols + side * side_cols
-        return out_ref.at[tok(k), pl.ds(pl.multiple_of(start, side_cols), side_cols)]
-
-    def oa_copy(k, r, c, columns_of):
-        return remote(
-            oa.at[k, c, pl.ds(r * t, t)], out_at(k, columns_of, 0), oa_sem, (k, r, c), down(r, 0)
-        )
-
-    def ob_copy(k, r, c, columns_of):
-        return remote(
-            ob.at[k, r, pl.ds(c * t, t)], out_at(k, columns_of, 1), ob_sem, (k, r, c), down(0, c)
-        )
-
-    def oa_own(k, c):
-        return pltpu.make_async_copy(
-            oa.at[k, c, pl.ds(0, t)], out_at(k, up(0, c), 0), oa_sem.at[1, k, 0, c]
-        )
-
-    def ob_own(k, r):
-        return pltpu.make_async_copy(
-            ob.at[k, r, pl.ds(0, t)], out_at(k, up(r, 0), 1), ob_sem.at[1, k, r, 0]
+        return remote(hb.at[0, tok(k)], hb.at[c, tok(k)], hb_sem, (k, c), up(0, c))
+
+    def columns(rc, side, start, width):
+        base = (rc[0] * cols + rc[1]) * 2 * side_cols + side * side_cols + start
+        return pl.ds(pl.multiple_of(base, width), width)
+
+    def oa_copy(k, r, columns_of):
+        return remote(
+            oa.at[0, r - 1, tok(k)], out_ref.at[tok(k), columns(columns_of, 0, 0, side_cols)],
+            oa_sem, (k, r), down(r, 0),
+        )
+
+    def ob_copy(k, c, columns_of):
+        return remote(
+            ob.at[0, c - 1, tok(k)], out_ref.at[tok(k), columns(columns_of, 1, 0, side_cols)],
+            ob_sem, (k, c), down(0, c),
+        )
+
+    out_tile = tile_of(side_cols, 256)
+    out_tiles = side_cols // out_tile
+
+    def ga_copy(c, j, r, columns_of):
+        return remote(
+            oa.at[c, r - 1, :, pl.ds(j * out_tile, out_tile)],
+            out_ref.at[:, columns(columns_of, 0, j * out_tile, out_tile)],
+            ga_sem, (c, j, r), down(r, 0),
+        )
+
+    def gb_copy(r, j, c, columns_of):
+        return remote(
+            ob.at[r, c - 1, :, pl.ds(j * out_tile, out_tile)],
+            out_ref.at[:, columns(columns_of, 1, j * out_tile, out_tile)],
+            gb_sem, (r, j, c), down(0, c),
         )
 
     loads = [
@@ -227,6 +246,7 @@
     for r, c in others:
         to = up(r, c)
         pl.semaphore_signal(barrier, inc=1, device_id={"row": to[0], "col": to[1]}, device_id_type=MESH)
+
     def greet(g):
         pl.semaphore_signal(barrier, inc=1, device_id={"dp": g}, device_id_type=MESH)
 
@@ -235,30 +255,29 @@
     if mates > 1:
         greet(plane * mates + (mates - 1 - core))
     neighbours = (plane > 0).astype(jnp.int32) + (plane + 1 < planes).astype(jnp.int32)
+    for k in range(chunks):
+        x_own(k).start()
+    for load in loads:
+        load.start()
     pl.semaphore_wait(barrier, n - 1 + mates - 1 + neighbours)
 
     for c in range(1, cols):
         fetch_a(c).start()
     for r in range(1, rows):
         fetch_b(r).start()
-
-    def send_tokens(k):
+    for k in range(chunks):
         for r, c in by_reach:
             x_copy(k, r, c).start()
 
-    for k in range(min(AHEAD, chunks)):
-        send_tokens(k)
-    for k in range(chunks):
-        x_own(k).start()
-    for load in loads:
-        load.start()
-    for c in range(1, cols):
-        fetch_a(c).wait_recv()
-    for r in range(1, rows):
-        fetch_b(r).wait_recv()
-    spread(plane, True, True)
-    for load in loads:
-        load.wait()
+    def fetch():
+        for c in range(1, cols):
+            fetch_a(c).wait_recv()
+        spread(plane, blocks_a, True, True)
+        for r in range(1, rows):
+            fetch_b(r).wait_recv()
+        spread(plane, blocks_b, True, True)
+        for load in loads:
+            load.wait()
 
     tile = tile_of(half, 512)
     per_half = half // tile
@@ -323,102 +342,139 @@
                     total = total + fin_b[k, r].astype(f32)
             gate = total[:, :half]
             done = (gate / (1.0 + jnp.exp(-gate)) * total[:, half:]).astype(bf16)
-            ha[k, pl.ds(0, t), pl.ds(side * half, half)] = done
-            hb[k, pl.ds(0, t), pl.ds(side * half, half)] = done
+            ha[0, tok(k), pl.ds(side * half, half)] = done
+            hb[0, tok(k), pl.ds(side * half, half)] = done
         for r in range(1, rows):
             ha_copy(k, r).start()
         for c in range(1, cols):
             hb_copy(k, c).start()
 
-    out_tile = tile_of(side_cols, 512)
-    out_tiles = side_cols // out_tile
+    wide = tile_of(side_cols, 512)
+    wides = side_cols // wide
 
     def emit(k):
         for r in range(1, rows):
             ha_copy(k, r).wait_recv()
-
-        def columns_a(j, _):
-            c = j // out_tiles
-            where = pl.ds(pl.multiple_of(lax.rem(j, out_tiles) * out_tile, out_tile), out_tile)
-            oa[k, c, :, where] = jnp.dot(
-                ha[k], wa[c, :, where], preferred_element_type=f32
-            ).astype(bf16)
+        theirs = ha[pl.ds(1, rows - 1), tok(k)].reshape((rows - 1) * t, hidden)
+        for j in range(wides):
+            where = pl.ds(j * wide, wide)
+            got = jnp.dot(theirs, wa[0, :, where], preferred_element_type=f32).astype(bf16)
+            oa[0, :, tok(k), where] = got.reshape(rows - 1, t, wide)
+        for r in range(1, rows):
+            oa_copy(k, r, (row, col)).start()
+        for c in range(1, cols):
+            hb_copy(k, c).wait_recv()
+        theirs = hb[pl.ds(1, cols - 1), tok(k)].reshape((cols - 1) * t, hidden)
+        for j in range(wides):
+            where = pl.ds(j * wide, wide)
+            got = jnp.dot(theirs, wb[0, :, where], preferred_element_type=f32).astype(bf16)
+            ob[0, :, tok(k), where] = got.reshape(cols - 1, t, wide)
+        for c in range(1, cols):
+            ob_copy(k, c, (row, col)).start()
+
+    def local():
+        def columns_of(j, _):
+            where = pl.ds(pl.multiple_of(j * wide, wide), wide)
+            for side, w in ((0, wa), (1, wb)):
+                out_ref[:, columns((row, col), side, j * wide, wide)] = jnp.dot(
+                    ha[0], w[0, :, where], preferred_element_type=f32
+                ).astype(bf16)
             return 0
 
-        lax.fori_loop(0, cols * out_tiles, columns_a, 0)
-        for c in range(cols):
-            for r in range(1, rows):
-                oa_copy(k, r, c, up(0, c)).start()
-        for c in range(1, cols):
-            hb_copy(k, c).wait_recv()
-
-        def columns_b(j, _):
-            r = j // out_tiles
-            where = pl.ds(pl.multiple_of(lax.rem(j, out_tiles) * out_tile, out_tile), out_tile)
-            ob[k, r, :, where] = jnp.dot(
-                hb[k], wb[r, :, where], preferred_element_type=f32
-            ).astype(bf16)
+        lax.fori_loop(0, wides, columns_of, 0)
+
+    count = t * chunks
+
+    def fetched_a(i):
+        c, j = 1 + i // out_tiles, lax.rem(i, out_tiles)
+        where = pl.ds(pl.multiple_of(j * out_tile, out_tile), out_tile)
+        got = jnp.dot(
+            ha[...].reshape(rows * count, hidden), wa[c, :, where], preferred_element_type=f32
+        ).astype(bf16)
+        oa[c, :, :, where] = got[count:].reshape(rows - 1, count, out_tile)
+        for r in range(1, rows):
+            ga_copy(c, j, r, up(0, c)).start()
+        out_ref[:, columns(up(0, c), 0, j * out_tile, out_tile)] = got[:count]
+
+    def fetched_b(i):
+        r, j = 1 + i // out_tiles, lax.rem(i, out_tiles)
+        where = pl.ds(pl.multiple_of(j * out_tile, out_tile), out_tile)
+        got = jnp.dot(
+            hb[...].reshape(cols * count, hidden), wb[r, :, where], preferred_element_type=f32
+        ).astype(bf16)
+        ob[r, :, :, where] = got[count:].reshape(cols - 1, count, out_tile)
+        for c in range(1, cols):
+            gb_copy(r, j, c, up(r, 0)).start()
+        out_ref[:, columns(up(r, 0), 1, j * out_tile, out_tile)] = got[:count]
+
+    tiles_a, tiles_b = (cols - 1) * out_tiles, (rows - 1) * out_tiles
+    both = min(tiles_a, tiles_b)
+
+    def emit_fetched():
+        def pair(i, _):
+            fetched_a(i)
+            fetched_b(i)
             return 0
 
-        lax.fori_loop(0, rows * out_tiles, columns_b, 0)
-        for r in range(rows):
-            for c in range(1, cols):
-                ob_copy(k, r, c, up(r, 0)).start()
-        for c in range(cols):
-            oa_own(k, c).start()
-        for r in range(rows):
-            ob_own(k, r).start()
-
-    stages = (project, combine, activate, emit)
-
-    def step(s, _):
-        for lag, stage in enumerate(stages):
-            k = s - lag
-
-            @pl.when(jnp.logical_and(k >= 0, k < chunks))
-            def _():
-                stage(k)
-
-            if lag == 0:
-
-                @pl.when(s + AHEAD < chunks)
-                def _():
-                    send_tokens(s + AHEAD)
-
-                for h in range(1, min(EARLY_HOPS, planes - 1) + 1):
-                    pl.when(s == h)(lambda h=h: hop(h))
-
-                pl.when(s == len(stages) - 1)(last_hops)
-
-        return 0
-
-    lax.fori_loop(0, chunks + len(stages) - 1, step, 0)
+        def only(one):
+            def body(i, _):
+                one(i)
+                return 0
+
+            return body
+
+        lax.fori_loop(0, both, pair, 0)
+        lax.fori_loop(both, tiles_a, only(fetched_a), 0)
+        lax.fori_loop(both, tiles_b, only(fetched_b), 0)
+
+    def both_hops(h):
+        hop(h, blocks_a)
+        hop(h, blocks_b)
+
+    stages = {"project": project, "combine": combine, "activate": activate, "emit": emit}
+    once = {
+        "fetch": fetch, "last hops": last_hops, "landed": landed, "local": local, "emit fetched": emit_fetched,
+    }
+    for task in ORDER:
+        if task in once:
+            once[task]()
+        else:
+            name, at = task.split()
+            if name == "hop":
+                if int(at) < planes:
+                    both_hops(int(at))
+            else:
+                stages[name](int(at))
 
     def finish(k, _):
         for r, c in others:
             x_copy(k, r, c).wait_send()
-        for r, c in slots:
-            if r:
-                oa_copy(k, r, c, up(0, c)).wait_send()
-                oa_copy(k, r, c, up(r, c)).wait_recv()
-            else:
-                oa_own(k, c).wait()
-            if c:
-                ob_copy(k, r, c, up(r, 0)).wait_send()
-                ob_copy(k, r, c, up(r, c)).wait_recv()
-            else:
-                ob_own(k, r).wait()
-        for r in range(1, rows):
+        for r in range(1, rows):
+            oa_copy(k, r, (row, col)).wait_send()
+            oa_copy(k, r, up(r, 0)).wait_recv()
             a_copy(k, r).wait_send()
             d_copy(k, r).wait_send()
             ha_copy(k, r).wait_send()
         for c in range(1, cols):
+            ob_copy(k, c, (row, col)).wait_send()
+            ob_copy(k, c, up(0, c)).wait_recv()
             b_copy(k, c).wait_send()
             c_copy(k, c).wait_send()
             hb_copy(k, c).wait_send()
         return 0
 
     lax.fori_loop(0, chunks, finish, 0)
+
+    def finish_fetched(j, _):
+        for c in range(1, cols):
+            for r in range(1, rows):
+                ga_copy(c, j, r, up(0, c)).wait_send()
+                ga_copy(c, j, r, up(r, c)).wait_recv()
+                gb_copy(r, j, c, up(r, 0)).wait_send()
+                gb_copy(r, j, c, up(r, c)).wait_recv()
+        return 0
+
+    lax.fori_loop(0, out_tiles, finish_fetched, 0)
     for c in range(1, cols):
         fetch_a(c).wait_send()
     for r in range(1, rows):
@@ -437,6 +493,7 @@
         side_cols = w_down.shape[1] // 2
         chunks = CHUNKS
         t = count // chunks
+        out_tiles = side_cols // tile_of(side_cols, 256)
         bf16 = jnp.bfloat16
         any_space = pl.BlockSpec(memory_space=pl.ANY)
 
@@ -445,9 +502,9 @@
 
         return pl.pallas_call(
             functools.partial(kernel, groups, rows, cols, chunks),
-            out_shape=jax.ShapeDtypeStruct((count, width), bf16),
+            out_shape=pltpu.VMEM((count, width), bf16),
             in_specs=[any_space] * 4,
-            out_specs=any_space,
+            out_specs=pl.BlockSpec(memory_space=pltpu.VMEM),
             scratch_shapes=[
                 pltpu.VMEM((features, hidden), bf16),
                 pltpu.VMEM((features, hidden), bf16),
@@ -462,10 +519,10 @@
                 pltpu.VMEM((chunks, rows, t, hidden), bf16),
                 pltpu.VMEM((chunks, cols, t, hidden), bf16),
                 pltpu.VMEM((chunks, rows, t, hidden), bf16),
-                pltpu.VMEM((chunks, rows * t, hidden), bf16),
-                pltpu.VMEM((chunks, cols * t, hidden), bf16),
-                pltpu.VMEM((chunks, cols, rows * t, side_cols), bf16),
-                pltpu.VMEM((chunks, rows, cols * t, side_cols), bf16),
+                pltpu.VMEM((rows, count, hidden), bf16),
+                pltpu.VMEM((cols, count, hidden), bf16),
+                pltpu.VMEM((cols, rows - 1, count, side_cols), bf16),
+                pltpu.VMEM((rows, cols - 1, count, side_cols), bf16),
                 pltpu.SemaphoreType.DMA((4,)),
                 pltpu.SemaphoreType.DMA((2, cols)),
                 pltpu.SemaphoreType.DMA((2, rows)),
@@ -474,7 +531,9 @@
                 pltpu.SemaphoreType.DMA((planes, cols + rows)),
                 pltpu.SemaphoreType.DMA((2, planes, cols + rows)),
                 sems(n), sems(rows), sems(cols), sems(cols), sems(rows),
-                sems(rows), sems(cols), sems(rows, cols), sems(rows, cols),
+                sems(rows), sems(cols), sems(rows), sems(cols),
+                pltpu.SemaphoreType.DMA((2, cols, out_tiles, rows)),
+                pltpu.SemaphoreType.DMA((2, rows, out_tiles, cols)),
             ],
             compiler_params=pltpu.CompilerParams(collective_id=0, has_side_effects=True),
         )(tokens, w_gate, w_up, w_down)

time: 75.1 us -> 71.3 us (0.949); the launches traced: 73.7 us -> 71.2 us
  local copies, waits for them, and re-layouts: 3.1 us -> 1.32 us
  Pallas kernels: 70.6 us -> 69.8 us
    unnamed x1, local copies, waits for them, and re-layouts: 3.1 us -> 1.32 us
    pallas_call x1, Pallas kernels: 70.6 us -> 69.8 us  [shards(): pl.pallas_call(functools.partial(kernel, groups, rows, cols, chunks), out...]
where the time goes in v1:
time: 71.3 us; the launch traced here: 71.2 us
  Pallas kernels  69.8 us (98%)
  local copies, waits for them, and re-layouts  1.32 us (2%)
    pallas_call x1, Pallas kernels, shards(): pl.pallas_call(functools.partial(kernel, groups, rows, cols, chunks), out...  69.8 us

profile of v1, /device:TPU:0, one launch (start us, length us, event | category | flops | bytes accessed | tf_op | source)
XLA Modules:
  0.0 71.2 jit_solution(3615962714746781814)
XLA Ops:
  0.0 69.8 %shard_map.46 = bf16[128,8192]{1,0:T(8,128)(2,1)S(1)} custom-call(bf16[128,8192]{1,0:T(8,128)(2,1)} %x_ref.1, bf16[2048,1024]{1,0:T(8,128)(2,1)} %wg_ref.1, bf16[2048,1024]{1,0:T(8,128)(2,1)} %wu_ref.1, bf16[1024,2048]{1,0:T(8,128)(2,1)} %wd_ref.1), custom_call_target="tpu_custom_call" | custom-call | tf_op jit(solution)/shard_map/pallas_call | solution.py:503
  69.9 1.3 %copy.6 = bf16[128,8192]{1,0:T(8,128)(2,1)} copy(bf16[128,8192]{1,0:T(8,128)(2,1)S(1)} %shard_map.46) | data formatting | bytes 4194304

commit v2 on v1

v2 whole, which is shorter than its diff:
```python
import functools

import jax
import jax.numpy as jnp
from jax import lax
from jax.experimental import pallas as pl
from jax.experimental.pallas import tpu as pltpu
from jax.sharding import PartitionSpec as P

MESH = pl.DeviceIdType.MESH
CHUNKS = 4
EARLY_HOPS = 2
ORDER = (
    "fetch", "project 0", "project 1", "hop 1", "project 2", "project 3", "hop 2", "combine 0", "combine 1",
    "combine 2", "combine 3", "activate 0", "activate 1", "activate 2", "activate 3", "emit 0", "emit 1",
    "last hops", "local", "emit 2", "emit 3", "landed", "emit fetched",
)
X, A, B, C, D, HA, HB, OA, OB, FA, FB, ZA, ZB, MA, MB = range(15)


def tile_of(width, most):
    tile = min(width, most)
    while width % tile:
        tile //= 2
    return tile


def kernel(
    groups, rows, cols, chunks,
    x_ref, wg_ref, wu_ref, wd_ref, out_ref,
    xin, wf, wg, wu, wa, wb, xbuf, acc, part, rec_a, rec_b, sum_a, sum_b, fin_a, fin_b, ha, hb, oa, ob,
    load_sem, sent_sem, x_sem, step_sem, fetch_sem, land_sem, mate_sem, out_sem,
):
    n = rows * cols
    row, col = lax.axis_index("row"), lax.axis_index("col")
    group = lax.axis_index("dp")
    mates = 2
    planes = groups // mates
    plane, core = group // mates, lax.rem(group, mates)
    count = x_ref.shape[0]
    t = count // chunks
    features, hidden = wg.shape
    half = hidden // 2
    side_cols = wa.shape[2]
    share = hidden // groups
    bf16, f32 = jnp.bfloat16, jnp.float32

    def up(r, c):
        return lax.rem(row + r, rows), lax.rem(col + c, cols)

    def down(r, c):
        return lax.rem(row + rows - r, rows), lax.rem(col + cols - c, cols)

    def shard(rc, width):
        return pl.ds(pl.multiple_of((rc[0] * cols + rc[1]) * width, width), width)

    def remote(src, dst, kind, landing, to):
        return pltpu.make_async_remote_copy(
            src_ref=src, dst_ref=dst, send_sem=sent_sem.at[kind], recv_sem=landing,
            device_id={"row": to[0], "col": to[1]}, device_id_type=MESH,
        )

    def all_sent(kind, ref):
        remote(ref, ref, kind, out_sem.at[0], up(rows - 1, cols - 1)).wait_send()

    def all_here(landing, ref):
        remote(ref, ref, 0, landing, up(rows - 1, cols - 1)).wait_recv()

    def tok(k):
        return pl.ds(k * t, t)

    others = [(r, c) for r in range(rows) for c in range(cols)][1:]
    by_reach = others[::-1]
    rest_rows, rest_cols = pl.ds(1, rows - 1), pl.ds(1, cols - 1)

    def x_copy(k, r, c):
        to = up(r, c)
        return remote(
            xin.at[tok(k), shard(to, features)], xbuf.at[k, pl.ds((r * cols + c) * t, t)], X, x_sem.at[k], to
        )

    def a_copy(k, r):
        return remote(part.at[k, 0, r], rec_a.at[k, r], A, step_sem.at[0, k], down(r, 0))

    def b_copy(k, c):
        return remote(part.at[k, 1, :, c], rec_b.at[k, c], B, step_sem.at[1, k], down(0, c))

    def c_copy(k, c):
        return remote(sum_a.at[k, c], fin_a.at[k, c], C, step_sem.at[2, k], down(0, c))

    def d_copy(k, r):
        return remote(sum_b.at[k, r], fin_b.at[k, r], D, step_sem.at[3, k], down(r, 0))

    def ha_copy(k, r):
        return remote(ha.at[0, tok(k)], ha.at[r, tok(k)], HA, step_sem.at[4, k], up(r, 0))

    def hb_copy(k, c):
        return remote(hb.at[0, tok(k)], hb.at[c, tok(k)], HB, step_sem.at[5, k], up(0, c))

    def share_of(g):
        return pl.ds(pl.multiple_of(g * share, share), share)

    def fetch_a(c):
        return remote(wf.at[0], wa.at[c, share_of(group)], FA, fetch_sem.at[0], down(0, c))

    def fetch_b(r):
        return remote(wf.at[1], wb.at[r, share_of(group)], FB, fetch_sem.at[1], down(r, 0))

    sides = ((wa, rest_cols), (wb, rest_rows))

    def pass_on(source, side, to_plane):
        ref, rest = sides[side]
        region = ref.at[rest, share_of(source * mates + core)]
        return pltpu.make_async_remote_copy(
            src_ref=region, dst_ref=region, send_sem=sent_sem.at[ZA + side], recv_sem=land_sem.at[source, side],
            device_id={"dp": to_plane * mates + core}, device_id_type=MESH,
        )

    def to_mate(source, side):
        ref, rest = sides[side]
        region = ref.at[rest, share_of(source * mates + core)]
        return pltpu.make_async_remote_copy(
            src_ref=region, dst_ref=region, send_sem=sent_sem.at[MA + side], recv_sem=mate_sem.at[side],
            device_id={"dp": plane * mates + (mates - 1 - core)}, device_id_type=MESH,
        )

    def spread(source, side, upward, downward):
        if upward:
            pl.when(plane + 1 < planes)(lambda: pass_on(source, side, plane + 1).start())
        if downward:
            pl.when(plane > 0)(lambda: pass_on(source, side, plane - 1).start())
        to_mate(source, side).start()

    def hop(h):
        below, above = plane - h, plane + h
        for side in range(2):

            @pl.when(below >= 0)
            def _():
                pass_on(below, side, plane).wait_recv()
                spread(below, side, True, False)

            @pl.when(above < planes)
            def _():
                pass_on(above, side, plane).wait_recv()
                spread(above, side, False, True)

    def last_hops():
        def more(h, _):
            hop(h)
            return 0

        lax.fori_loop(EARLY_HOPS + 1, planes, more, 0)

    def landed():
        for side, (ref, rest) in enumerate(sides):
            all_here(mate_sem.at[side], ref.at[rest, pl.ds(0, planes * share)])

    def columns(rc, side, start, width):
        base = (rc[0] * cols + rc[1]) * 2 * side_cols + side * side_cols + start
        return pl.ds(pl.multiple_of(base, width), width)

    def oa_copy(k, r):
        return remote(
            oa.at[0, r - 1, tok(k)], out_ref.at[tok(k), columns((row, col), 0, 0, side_cols)],
            OA, out_sem.at[0], down(r, 0),
        )

    def ob_copy(k, c):
        return remote(
            ob.at[0, c - 1, tok(k)], out_ref.at[tok(k), columns((row, col), 1, 0, side_cols)],
            OB, out_sem.at[1], down(0, c),
        )

    out_tile = tile_of(side_cols, 256)
    out_tiles = side_cols // out_tile

    def ga_copy(c, j, r):
        return remote(
            oa.at[c, r - 1, :, pl.ds(pl.multiple_of(j * out_tile, out_tile), out_tile)],
            out_ref.at[:, columns(up(0, c), 0, j * out_tile, out_tile)],
            OA, out_sem.at[0], down(r, 0),
        )

    def gb_copy(r, j, c):
        return remote(
            ob.at[r, c - 1, :, pl.ds(pl.multiple_of(j * out_tile, out_tile), out_tile)],
            out_ref.at[:, columns(up(r, 0), 1, j * out_tile, out_tile)],
            OB, out_sem.at[1], down(0, c),
        )

    own_share = share_of(group)
    first_loads = [
        pltpu.make_async_copy(wd_ref.at[own_share, pl.ds(0, side_cols)], wf.at[0], load_sem.at[0]),
        pltpu.make_async_copy(wd_ref.at[own_share, pl.ds(side_cols, side_cols)], wf.at[1], load_sem.at[1]),
        pltpu.make_async_copy(x_ref, xin, load_sem.at[2]),
    ]
    own = [
        pltpu.make_async_copy(
            x_ref.at[tok(k), shard((row, col), features)], xbuf.at[k, pl.ds(0, t)], load_sem.at[3 + k]
        )
        for k in range(chunks)
    ]
    loads = [
        pltpu.make_async_copy(wg_ref, wg, load_sem.at[3 + chunks]),
        pltpu.make_async_copy(wu_ref, wu, load_sem.at[4 + chunks]),
        pltpu.make_async_copy(wd_ref.at[:, pl.ds(0, side_cols)], wa.at[0], load_sem.at[5 + chunks]),
        pltpu.make_async_copy(wd_ref.at[:, pl.ds(side_cols, side_cols)], wb.at[0], load_sem.at[6 + chunks]),
    ]

    barrier = pltpu.get_barrier_semaphore()
    for r, c in others:
        to = up(r, c)
        pl.semaphore_signal(barrier, inc=1, device_id={"row": to[0], "col": to[1]}, device_id_type=MESH)

    def greet(g):
        pl.semaphore_signal(barrier, inc=1, device_id={"dp": g}, device_id_type=MESH)

    pl.when(plane > 0)(lambda: greet(group - mates))
    pl.when(plane + 1 < planes)(lambda: greet(group + mates))
    greet(plane * mates + (mates - 1 - core))
    neighbours = (plane > 0).astype(jnp.int32) + (plane + 1 < planes).astype(jnp.int32)
    for load in first_loads:
        load.start()
    for load in first_loads:
        load.wait()
    pl.semaphore_wait(barrier, n - 1 + mates - 1 + neighbours)

    for c in range(1, cols):
        fetch_a(c).start()
    for r in range(1, rows):
        fetch_b(r).start()
    for k in range(chunks):
        for r, c in by_reach:
            x_copy(k, r, c).start()
    for load in own + loads:
        load.start()

    def fetch():
        all_here(fetch_sem.at[0], wa.at[rest_cols, own_share])
        spread(plane, 0, True, True)
        all_here(fetch_sem.at[1], wb.at[rest_rows, own_share])
        spread(plane, 1, True, True)
        for load in loads:
            load.wait()

    tile = tile_of(half, 512)
    per_half = half // tile

    def project(k):
        own[k].wait()
        all_here(x_sem.at[k], xbuf.at[k, pl.ds(t, (n - 1) * t)])

        def column(j, _):
            side, at = j // per_half, lax.rem(j, per_half) * tile
            source = pl.ds(pl.multiple_of(j * tile, tile), tile)
            for w, base in ((wg, 0), (wu, half)):
                target = pl.ds(pl.multiple_of(base + at, tile), tile)
                got = jnp.dot(xbuf[k], w[:, source], preferred_element_type=f32)
                acc[k, side, :, target] = got[:t]
                for r, c in others:
                    first = (r * cols + c) * t
                    part[k, side, r, c, :, target] = got[first : first + t].astype(bf16)
            return 0

        lax.fori_loop(0, 2 * per_half, column, 0)
        for r in range(1, rows):
            a_copy(k, r).start()
        for c in range(1, cols):
            b_copy(k, c).start()

    def combine(k):
        all_here(step_sem.at[0, k], rec_a.at[k, rest_rows])
        for c in range(1, cols):
            total = part[k, 0, 0, c].astype(f32)
            for r in range(1, rows):
                total = total + rec_a[k, r, c].astype(f32)
            sum_a[k, c] = total.astype(bf16)
            c_copy(k, c).start()
        all_here(step_sem.at[1, k], rec_b.at[k, rest_cols])
        for r in range(1, rows):
            total = part[k, 1, r, 0].astype(f32)
            for c in range(1, cols):
                total = total + rec_b[k, c, r].astype(f32)
            sum_b[k, r] = total.astype(bf16)
            d_copy(k, r).start()

    def activate(k):
        all_here(step_sem.at[2, k], fin_a.at[k, rest_cols])
        all_here(step_sem.at[3, k], fin_b.at[k, rest_rows])
        for side in range(2):
            total = acc[k, side]
            if side == 0:
                for r in range(1, rows):
                    total = total + rec_a[k, r, 0].astype(f32)
                for c in range(1, cols):
                    total = total + fin_a[k, c].astype(f32)
            else:
                for c in range(1, cols):
                    total = total + rec_b[k, c, 0].astype(f32)
                for r in range(1, rows):
                    total = total + fin_b[k, r].astype(f32)
            gate = total[:, :half]
            done = (gate / (1.0 + jnp.exp(-gate)) * total[:, half:]).astype(bf16)
            ha[0, tok(k), pl.ds(side * half, half)] = done
            hb[0, tok(k), pl.ds(side * half, half)] = done
        for r in range(1, rows):
            ha_copy(k, r).start()
        for c in range(1, cols):
            hb_copy(k, c).start()

    wide = tile_of(side_cols, 512)
    wides = side_cols // wide

    def emit(k):
        all_here(step_sem.at[4, k], ha.at[rest_rows, tok(k)])
        theirs = ha[rest_rows, tok(k)].reshape((rows - 1) * t, hidden)
        for j in range(wides):
            where = pl.ds(j * wide, wide)
            got = jnp.dot(theirs, wa[0, :, where], preferred_element_type=f32).astype(bf16)
            oa[0, :, tok(k), where] = got.reshape(rows - 1, t, wide)
        for r in range(1, rows):
            oa_copy(k, r).start()
        all_here(step_sem.at[5, k], hb.at[rest_cols, tok(k)])
        theirs = hb[rest_cols, tok(k)].reshape((cols - 1) * t, hidden)
        for j in range(wides):
            where = pl.ds(j * wide, wide)
            got = jnp.dot(theirs, wb[0, :, where], preferred_element_type=f32).astype(bf16)
            ob[0, :, tok(k), where] = got.reshape(cols - 1, t, wide)
        for c in range(1, cols):
            ob_copy(k, c).start()

    def local():
        def columns_of(j, _):
            where = pl.ds(pl.multiple_of(j * wide, wide), wide)
            for side, w in ((0, wa), (1, wb)):
                out_ref[:, columns((row, col), side, j * wide, wide)] = jnp.dot(
                    ha[0], w[0, :, where], preferred_element_type=f32
                ).astype(bf16)
            return 0

        lax.fori_loop(0, wides, columns_of, 0)

    def fetched_a(i):
        c, j = 1 + i // out_tiles, lax.rem(i, out_tiles)
        where = pl.ds(pl.multiple_of(j * out_tile, out_tile), out_tile)
        got = jnp.dot(
            ha[...].reshape(rows * count, hidden), wa[c, :, where], preferred_element_type=f32
        ).astype(bf16)
        oa[c, :, :, where] = got[count:].reshape(rows - 1, count, out_tile)
        for r in range(1, rows):
            ga_copy(c, j, r).start()
        out_ref[:, columns(up(0, c), 0, j * out_tile, out_tile)] = got[:count]

    def fetched_b(i):
        r, j = 1 + i // out_tiles, lax.rem(i, out_tiles)
        where = pl.ds(pl.multiple_of(j * out_tile, out_tile), out_tile)
        got = jnp.dot(
            hb[...].reshape(cols * count, hidden), wb[r, :, where], preferred_element_type=f32
        ).astype(bf16)
        ob[r, :, :, where] = got[count:].reshape(cols - 1, count, out_tile)
        for c in range(1, cols):
            gb_copy(r, j, c).start()
        out_ref[:, columns(up(r, 0), 1, j * out_tile, out_tile)] = got[:count]

    tiles_a, tiles_b = (cols - 1) * out_tiles, (rows - 1) * out_tiles
    both = min(tiles_a, tiles_b)

    def emit_fetched():
        def pair(i, _):
            fetched_a(i)
            fetched_b(i)
            return 0

        def only(one):
            def body(i, _):
                one(i)
                return 0

            return body

        lax.fori_loop(0, both, pair, 0)
        lax.fori_loop(both, tiles_a, only(fetched_a), 0)
        lax.fori_loop(both, tiles_b, only(fetched_b), 0)

    stages = {"project": project, "combine": combine, "activate": activate, "emit": emit}
    once = {
        "fetch": fetch, "last hops": last_hops, "landed": landed, "local": local, "emit fetched": emit_fetched,
    }
    for task in ORDER:
        if task in once:
            once[task]()
        else:
            name, at = task.split()
            if name == "hop":
                if int(at) < planes:
                    hop(int(at))
            else:
                stages[name](int(at))

    all_sent(X, xbuf.at[:, pl.ds(t, (n - 1) * t)])
    all_sent(A, rec_a.at[:, rest_rows])
    all_sent(B, rec_b.at[:, rest_cols])
    all_sent(C, fin_a.at[:, rest_cols])
    all_sent(D, fin_b.at[:, rest_rows])
    all_sent(HA, ha.at[rest_rows])
    all_sent(HB, hb.at[rest_cols])
    all_sent(FA, wa.at[rest_cols, own_share])
    all_sent(FB, wb.at[rest_rows, own_share])
    for side, (ref, rest) in enumerate(sides):
        all_sent(MA + side, ref.at[rest, pl.ds(0, planes * share)])
        if planes > 1:
            inner = jnp.logical_and(plane > 0, plane + 1 < planes)
            pl.when(inner)(lambda: all_sent(ZA + side, ref.at[rest, pl.ds(0, (planes + 1) * share)]))
            pl.when(jnp.logical_not(inner))(lambda: all_sent(ZA + side, ref.at[rest, pl.ds(0, share)]))
    all_sent(OA, oa)
    all_sent(OB, ob)
    all_here(out_sem.at[0], oa)
    all_here(out_sem.at[1], ob)


def solution(mesh):
    groups, rows, cols = mesh.shape["dp"], mesh.shape["row"], mesh.shape["col"]
    planes = groups // 2
    n = rows * cols

    def shards(tokens, w_gate, w_up, w_down):
        count, width = tokens.shape
        features, hidden = w_gate.shape
        side_cols = w_down.shape[1] // 2
        chunks = CHUNKS
        t = count // chunks
        bf16 = jnp.bfloat16
        any_space = pl.BlockSpec(memory_space=pl.ANY)
        dma = pltpu.SemaphoreType.DMA

        return pl.pallas_call(
            functools.partial(kernel, groups, rows, cols, chunks),
            out_shape=pltpu.VMEM((count, width), bf16),
            in_specs=[any_space] * 4,
            out_specs=pl.BlockSpec(memory_space=pltpu.VMEM),
            scratch_shapes=[
                pltpu.VMEM((count, width), bf16),
                pltpu.VMEM((2, hidden // groups, side_cols), bf16),
                pltpu.VMEM((features, hidden), bf16),
                pltpu.VMEM((features, hidden), bf16),
                pltpu.VMEM((cols, hidden, side_cols), bf16),
                pltpu.VMEM((rows, hidden, side_cols), bf16),
                pltpu.VMEM((chunks, n * t, features), bf16),
                pltpu.VMEM((chunks, 2, t, hidden), jnp.float32),
                pltpu.VMEM((chunks, 2, rows, cols, t, hidden), bf16),
                pltpu.VMEM((chunks, rows, cols, t, hidden), bf16),
                pltpu.VMEM((chunks, cols, rows, t, hidden), bf16),
                pltpu.VMEM((chunks, cols, t, hidden), bf16),
                pltpu.VMEM((chunks, rows, t, hidden), bf16),
                pltpu.VMEM((chunks, cols, t, hidden), bf16),
                pltpu.VMEM((chunks, rows, t, hidden), bf16),
                pltpu.VMEM((rows, count, hidden), bf16),
                pltpu.VMEM((cols, count, hidden), bf16),
                pltpu.VMEM((cols, rows - 1, count, side_cols), bf16),
                pltpu.VMEM((rows, cols - 1, count, side_cols), bf16),
                dma((7 + chunks,)),
                dma((15,)),
                dma((chunks,)),
                dma((6, chunks)),
                dma((2,)),
                dma((planes, 2)),
                dma((2,)),
                dma((2,)),
            ],
            compiler_params=pltpu.CompilerParams(collective_id=0, has_side_effects=True),
        )(tokens, w_gate, w_up, w_down)

    in_specs = (
        P(("dp", "row", "col"), None),
        P(("row", "col"), None),
        P(("row", "col"), None),
        P(None, ("row", "col")),
    )
    out_specs = P(("dp", "row", "col"), None)
    return jax.shard_map(shards, mesh=mesh, in_specs=in_specs, out_specs=out_specs, check_vma=False)
```

time: 71.3 us -> 69.5 us (0.975)
  Pallas kernels: 69.8 us -> 68 us
    pallas_call x1, Pallas kernels: 69.8 us -> 68 us  [shards(): pl.pallas_call(functools.partial(kernel, groups, rows, cols, chunks), out...]
where the time goes in v2:
time: 69.5 us; the launch traced here: 69.3 us
  Pallas kernels  68 us (98%)
  local copies, waits for them, and re-layouts  1.32 us (2%)
    pallas_call x1, Pallas kernels, shards(): pl.pallas_call(functools.partial(kernel, groups, rows, cols, chunks), out...  68 us

profile of v2, /device:TPU:0, one launch (start us, length us, event | category | flops | bytes accessed | tf_op | source)
XLA Modules:
  0.0 69.3 jit_solution(3883620756956539258)
XLA Ops:
  0.0 68.0 %shard_map.46 = bf16[128,8192]{1,0:T(8,128)(2,1)S(1)} custom-call(bf16[128,8192]{1,0:T(8,128)(2,1)} %x_ref.1, bf16[2048,1024]{1,0:T(8,128)(2,1)} %wg_ref.1, bf16[2048,1024]{1,0:T(8,128)(2,1)} %wu_ref.1, bf16[1024,2048]{1,0:T(8,128)(2,1)} %wd_ref.1), custom_call_target="tpu_custom_call" | custom-call | tf_op jit(solution)/shard_map/pallas_call | solution.py:437
  68.0 1.3 %copy.6 = bf16[128,8192]{1,0:T(8,128)(2,1)} copy(bf16[128,8192]{1,0:T(8,128)(2,1)S(1)} %shard_map.46) | data formatting | bytes 4194304

commit v3 on v2

--- a/solution.py
+++ b/solution.py
@@ -208,6 +208,9 @@
         pltpu.make_async_copy(wd_ref.at[:, pl.ds(side_cols, side_cols)], wb.at[0], load_sem.at[6 + chunks]),
     ]
 
+    for load in first_loads:
+        load.start()
+
     barrier = pltpu.get_barrier_semaphore()
     for r, c in others:
         to = up(r, c)
@@ -220,9 +223,7 @@
     pl.when(plane + 1 < planes)(lambda: greet(group + mates))
     greet(plane * mates + (mates - 1 - core))
     neighbours = (plane > 0).astype(jnp.int32) + (plane + 1 < planes).astype(jnp.int32)
-    for load in first_loads:
-        load.start()
-    for load in first_loads:
+    for load in first_loads[:2]:
         load.wait()
     pl.semaphore_wait(barrier, n - 1 + mates - 1 + neighbours)
 
@@ -230,6 +231,7 @@
         fetch_a(c).start()
     for r in range(1, rows):
         fetch_b(r).start()
+    first_loads[2].wait()
     for k in range(chunks):
         for r, c in by_reach:
             x_copy(k, r, c).start()

time: 69.5 us -> 68.9 us (level)
  no operation moved by 1% of the time
where the time goes in v3:
time: 68.9 us; the launch traced here: 68.7 us
  Pallas kernels  67.4 us (98%)
  local copies, waits for them, and re-layouts  1.32 us (2%)
    pallas_call x1, Pallas kernels, shards(): pl.pallas_call(functools.partial(kernel, groups, rows, cols, chunks), out...  67.4 us

profile of v3, /device:TPU:0, one launch (start us, length us, event | category | flops | bytes accessed | tf_op | source)
XLA Modules:
  0.0 68.7 jit_solution(5515729954642886177)
XLA Ops:
  0.0 67.4 %shard_map.46 = bf16[128,8192]{1,0:T(8,128)(2,1)S(1)} custom-call(bf16[128,8192]{1,0:T(8,128)(2,1)} %x_ref.1, bf16[2048,1024]{1,0:T(8,128)(2,1)} %wg_ref.1, bf16[2048,1024]{1,0:T(8,128)(2,1)} %wu_ref.1, bf16[1024,2048]{1,0:T(8,128)(2,1)} %wd_ref.1), custom_call_target="tpu_custom_call" | custom-call | tf_op jit(solution)/shard_map/pallas_call | solution.py:439
  67.4 1.3 %copy.6 = bf16[128,8192]{1,0:T(8,128)(2,1)} copy(bf16[128,8192]{1,0:T(8,128)(2,1)S(1)} %shard_map.46) | data formatting | bytes 4194304

commit v4 on v2

--- a/solution.py
+++ b/solution.py
@@ -1,4 +1,5 @@
 import functools
+import math
 
 import jax
 import jax.numpy as jnp
@@ -9,6 +10,7 @@
 
 MESH = pl.DeviceIdType.MESH
 CHUNKS = 4
+SMALL_PART = 5, 16
 EARLY_HOPS = 2
 ORDER = (
     "fetch", "project 0", "project 1", "hop 1", "project 2", "project 3", "hop 2", "combine 0", "combine 1",
@@ -23,6 +25,10 @@
     while width % tile:
         tile //= 2
     return tile
+
+
+def small_share(pair):
+    return max(16, pair * SMALL_PART[0] // SMALL_PART[1] // 16 * 16)
 
 
 def kernel(
@@ -42,7 +48,8 @@
     features, hidden = wg.shape
     half = hidden // 2
     side_cols = wa.shape[2]
-    share = hidden // groups
+    pair = mates * hidden // groups
+    small = small_share(pair)
     bf16, f32 = jnp.bfloat16, jnp.float32
 
     def up(r, c):
@@ -97,53 +104,71 @@
     def hb_copy(k, c):
         return remote(hb.at[0, tok(k)], hb.at[c, tok(k)], HB, step_sem.at[5, k], up(0, c))
 
-    def share_of(g):
-        return pl.ds(pl.multiple_of(g * share, share), share)
-
-    def fetch_a(c):
-        return remote(wf.at[0], wa.at[c, share_of(group)], FA, fetch_sem.at[0], down(0, c))
-
-    def fetch_b(r):
-        return remote(wf.at[1], wb.at[r, share_of(group)], FB, fetch_sem.at[1], down(r, 0))
+    share_sizes = (small, pair - small)
+
+    def share_of(source, m):
+        start = source * pair + (small if m else 0)
+        return pl.ds(pl.multiple_of(start, math.gcd(pair, small)), share_sizes[m])
+
+    def as_core(do):
+        for m in range(mates):
+
+            @pl.when(core == m)
+            def _():
+                do(m)
+
+    def fetch_a(m, c):
+        return remote(
+            wf.at[0, pl.ds(0, share_sizes[m])], wa.at[c, share_of(plane, m)], FA, fetch_sem.at[0], down(0, c)
+        )
+
+    def fetch_b(m, r):
+        return remote(
+            wf.at[1, pl.ds(0, share_sizes[m])], wb.at[r, share_of(plane, m)], FB, fetch_sem.at[1], down(r, 0)
+        )
 
     sides = ((wa, rest_cols), (wb, rest_rows))
 
-    def pass_on(source, side, to_plane):
+    def pass_on(source, side, m, to_plane):
         ref, rest = sides[side]
-        region = ref.at[rest, share_of(source * mates + core)]
+        region = ref.at[rest, share_of(source, m)]
         return pltpu.make_async_remote_copy(
             src_ref=region, dst_ref=region, send_sem=sent_sem.at[ZA + side], recv_sem=land_sem.at[source, side],
             device_id={"dp": to_plane * mates + core}, device_id_type=MESH,
         )
 
-    def to_mate(source, side):
+    def to_mate(source, side, m):
         ref, rest = sides[side]
-        region = ref.at[rest, share_of(source * mates + core)]
+        region = ref.at[rest, share_of(source, m)]
         return pltpu.make_async_remote_copy(
             src_ref=region, dst_ref=region, send_sem=sent_sem.at[MA + side], recv_sem=mate_sem.at[side],
             device_id={"dp": plane * mates + (mates - 1 - core)}, device_id_type=MESH,
         )
 
-    def spread(source, side, upward, downward):
+    def spread(source, side, m, upward, downward):
         if upward:
-            pl.when(plane + 1 < planes)(lambda: pass_on(source, side, plane + 1).start())
+            pl.when(plane + 1 < planes)(lambda: pass_on(source, side, m, plane + 1).start())
         if downward:
-            pl.when(plane > 0)(lambda: pass_on(source, side, plane - 1).start())
-        to_mate(source, side).start()
+            pl.when(plane > 0)(lambda: pass_on(source, side, m, plane - 1).start())
+        to_mate(source, side, m).start()
 
     def hop(h):
         below, above = plane - h, plane + h
-        for side in range(2):
-
-            @pl.when(below >= 0)
-            def _():
-                pass_on(below, side, plane).wait_recv()
-                spread(below, side, True, False)
-
-            @pl.when(above < planes)
-            def _():
-                pass_on(above, side, plane).wait_recv()
-                spread(above, side, False, True)
+
+        def relay(m):
+            for side in range(2):
+
+                @pl.when(below >= 0)
+                def _():
+                    pass_on(below, side, m, plane).wait_recv()
+                    spread(below, side, m, True, False)
+
+                @pl.when(above < planes)
+                def _():
+                    pass_on(above, side, m, plane).wait_recv()
+                    spread(above, side, m, False, True)
+
+        as_core(relay)
 
     def last_hops():
         def more(h, _):
@@ -153,8 +178,11 @@
         lax.fori_loop(EARLY_HOPS + 1, planes, more, 0)
 
     def landed():
-        for side, (ref, rest) in enumerate(sides):
-            all_here(mate_sem.at[side], ref.at[rest, pl.ds(0, planes * share)])
+        def from_mate(m):
+            for side, (ref, rest) in enumerate(sides):
+                all_here(mate_sem.at[side], ref.at[rest, pl.ds(0, planes * share_sizes[1 - m])])
+
+        as_core(from_mate)
 
     def columns(rc, side, start, width):
         base = (rc[0] * cols + rc[1]) * 2 * side_cols + side * side_cols + start
@@ -189,12 +217,16 @@
             OB, out_sem.at[1], down(0, c),
         )
 
-    own_share = share_of(group)
-    first_loads = [
-        pltpu.make_async_copy(wd_ref.at[own_share, pl.ds(0, side_cols)], wf.at[0], load_sem.at[0]),
-        pltpu.make_async_copy(wd_ref.at[own_share, pl.ds(side_cols, side_cols)], wf.at[1], load_sem.at[1]),
-        pltpu.make_async_copy(x_ref, xin, load_sem.at[2]),
-    ]
+    def load_share(m):
+        return [
+            pltpu.make_async_copy(
+                wd_ref.at[share_of(plane, m), pl.ds(side * side_cols, side_cols)],
+                wf.at[side, pl.ds(0, share_sizes[m])], load_sem.at[side],
+            )
+            for side in range(2)
+        ]
+
+    load_tokens = pltpu.make_async_copy(x_ref, xin, load_sem.at[2])
     own = [
         pltpu.make_async_copy(
             x_ref.at[tok(k), shard((row, col), features)], xbuf.at[k, pl.ds(0, t)], load_sem.at[3 + k]
@@ -208,6 +240,9 @@
         pltpu.make_async_copy(wd_ref.at[:, pl.ds(side_cols, side_cols)], wb.at[0], load_sem.at[6 + chunks]),
     ]
 
+    as_core(lambda m: [load.start() for load in load_share(m)])
+    load_tokens.start()
+
     barrier = pltpu.get_barrier_semaphore()
     for r, c in others:
         to = up(r, c)
@@ -220,16 +255,17 @@
     pl.when(plane + 1 < planes)(lambda: greet(group + mates))
     greet(plane * mates + (mates - 1 - core))
     neighbours = (plane > 0).astype(jnp.int32) + (plane + 1 < planes).astype(jnp.int32)
-    for load in first_loads:
-        load.start()
-    for load in first_loads:
-        load.wait()
+    as_core(lambda m: [load.wait() for load in load_share(m)])
     pl.semaphore_wait(barrier, n - 1 + mates - 1 + neighbours)
 
-    for c in range(1, cols):
-        fetch_a(c).start()
-    for r in range(1, rows):
-        fetch_b(r).start()
+    def send_share(m):
+        for c in range(1, cols):
+            fetch_a(m, c).start()
+        for r in range(1, rows):
+            fetch_b(m, r).start()
+
+    as_core(send_share)
+    load_tokens.wait()
     for k in range(chunks):
         for r, c in by_reach:
             x_copy(k, r, c).start()
@@ -237,10 +273,12 @@
         load.start()
 
     def fetch():
-        all_here(fetch_sem.at[0], wa.at[rest_cols, own_share])
-        spread(plane, 0, True, True)
-        all_here(fetch_sem.at[1], wb.at[rest_rows, own_share])
-        spread(plane, 1, True, True)
+        def take(m):
+            for side, (ref, rest) in enumerate(sides):
+                all_here(fetch_sem.at[side], ref.at[rest, share_of(plane, m)])
+                spread(plane, side, m, True, True)
+
+        as_core(take)
         for load in loads:
             load.wait()
 
@@ -348,9 +386,9 @@
             ha[...].reshape(rows * count, hidden), wa[c, :, where], preferred_element_type=f32
         ).astype(bf16)
         oa[c, :, :, where] = got[count:].reshape(rows - 1, count, out_tile)
+        out_ref[:, columns(up(0, c), 0, j * out_tile, out_tile)] = got[:count]
         for r in range(1, rows):
             ga_copy(c, j, r).start()
-        out_ref[:, columns(up(0, c), 0, j * out_tile, out_tile)] = got[:count]
 
     def fetched_b(i):
         r, j = 1 + i // out_tiles, lax.rem(i, out_tiles)
@@ -359,9 +397,9 @@
             hb[...].reshape(cols * count, hidden), wb[r, :, where], preferred_element_type=f32
         ).astype(bf16)
         ob[r, :, :, where] = got[count:].reshape(cols - 1, count, out_tile)
+        out_ref[:, columns(up(r, 0), 1, j * out_tile, out_tile)] = got[:count]
         for c in range(1, cols):
             gb_copy(r, j, c).start()
-        out_ref[:, columns(up(r, 0), 1, j * out_tile, out_tile)] = got[:count]
 
     tiles_a, tiles_b = (cols - 1) * out_tiles, (rows - 1) * out_tiles
     both = min(tiles_a, tiles_b)
@@ -405,14 +443,18 @@
     all_sent(D, fin_b.at[:, rest_rows])
     all_sent(HA, ha.at[rest_rows])
     all_sent(HB, hb.at[rest_cols])
-    all_sent(FA, wa.at[rest_cols, own_share])
-    all_sent(FB, wb.at[rest_rows, own_share])
-    for side, (ref, rest) in enumerate(sides):
-        all_sent(MA + side, ref.at[rest, pl.ds(0, planes * share)])
-        if planes > 1:
-            inner = jnp.logical_and(plane > 0, plane + 1 < planes)
-            pl.when(inner)(lambda: all_sent(ZA + side, ref.at[rest, pl.ds(0, (planes + 1) * share)]))
-            pl.when(jnp.logical_not(inner))(lambda: all_sent(ZA + side, ref.at[rest, pl.ds(0, share)]))
+
+    def shares_sent(m):
+        size = share_sizes[m]
+        for side, (ref, rest) in enumerate(sides):
+            all_sent(FA + side, ref.at[rest, pl.ds(0, size)])
+            all_sent(MA + side, ref.at[rest, pl.ds(0, planes * size)])
+            if planes > 1:
+                inner = jnp.logical_and(plane > 0, plane + 1 < planes)
+                pl.when(inner)(lambda: all_sent(ZA + side, ref.at[rest, pl.ds(0, (planes + 1) * size)]))
+                pl.when(jnp.logical_not(inner))(lambda: all_sent(ZA + side, ref.at[rest, pl.ds(0, size)]))
+
+    as_core(shares_sent)
     all_sent(OA, oa)
     all_sent(OB, ob)
     all_here(out_sem.at[0], oa)
@@ -428,6 +470,7 @@
         count, width = tokens.shape
         features, hidden = w_gate.shape
         side_cols = w_down.shape[1] // 2
+        pair = 2 * hidden // groups
         chunks = CHUNKS
         t = count // chunks
         bf16 = jnp.bfloat16
@@ -441,7 +484,7 @@
             out_specs=pl.BlockSpec(memory_space=pltpu.VMEM),
             scratch_shapes=[
                 pltpu.VMEM((count, width), bf16),
-                pltpu.VMEM((2, hidden // groups, side_cols), bf16),
+                pltpu.VMEM((2, pair - small_share(pair), side_cols), bf16),
                 pltpu.VMEM((features, hidden), bf16),
                 pltpu.VMEM((features, hidden), bf16),
                 pltpu.VMEM((cols, hidden, side_cols), bf16),

time: 69.5 us -> 68.2 us (0.981)
  Pallas kernels: 68 us -> 66.6 us
    pallas_call x1, Pallas kernels: 68 us -> 66.6 us  [shards(): pl.pallas_call(functools.partial(kernel, groups, rows, cols, chunks), out...]
where the time goes in v4:
time: 68.2 us; the launch traced here: 68 us
  Pallas kernels  66.6 us (98%)
  local copies, waits for them, and re-layouts  1.32 us (2%)
    pallas_call x1, Pallas kernels, shards(): pl.pallas_call(functools.partial(kernel, groups, rows, cols, chunks), out...  66.6 us

profile of v4, /device:TPU:0, one launch (start us, length us, event | category | flops | bytes accessed | tf_op | source)
XLA Modules:
  0.0 68.0 jit_solution(1801126895459925542)
XLA Ops:
  0.0 66.6 %shard_map.46 = bf16[128,8192]{1,0:T(8,128)(2,1)S(1)} custom-call(bf16[128,8192]{1,0:T(8,128)(2,1)} %x_ref.1, bf16[2048,1024]{1,0:T(8,128)(2,1)} %wg_ref.1, bf16[2048,1024]{1,0:T(8,128)(2,1)} %wu_ref.1, bf16[1024,2048]{1,0:T(8,128)(2,1)} %wd_ref.1), custom_call_target="tpu_custom_call" | custom-call | tf_op jit(solution)/shard_map/pallas_call | solution.py:480
  66.6 1.3 %copy.6 = bf16[128,8192]{1,0:T(8,128)(2,1)} copy(bf16[128,8192]{1,0:T(8,128)(2,1)S(1)} %shard_map.46) | data formatting | bytes 4194304

commit v5 on v4

--- a/solution.py
+++ b/solution.py
@@ -1,5 +1,4 @@
 import functools
-import math
 
 import jax
 import jax.numpy as jnp
@@ -11,6 +10,7 @@
 MESH = pl.DeviceIdType.MESH
 CHUNKS = 4
 SMALL_PART = 5, 16
+LATER_PART = 16
 EARLY_HOPS = 2
 ORDER = (
     "fetch", "project 0", "project 1", "hop 1", "project 2", "project 3", "hop 2", "combine 0", "combine 1",
@@ -27,8 +27,14 @@
     return tile
 
 
-def small_share(pair):
-    return max(16, pair * SMALL_PART[0] // SMALL_PART[1] // 16 * 16)
+def share_table(hidden, planes):
+    even = hidden // planes
+    later = even + even // LATER_PART // 16 * 16
+    table = []
+    for rows in (hidden - (planes - 1) * later, later):
+        small = max(16, rows * SMALL_PART[0] // SMALL_PART[1] // 16 * 16)
+        table.append((small, rows - small))
+    return table
 
 
 def kernel(
@@ -48,8 +54,7 @@
     features, hidden = wg.shape
     half = hidden // 2
     side_cols = wa.shape[2]
-    pair = mates * hidden // groups
-    small = small_share(pair)
+    sizes = share_table(hidden, planes)
     bf16, f32 = jnp.bfloat16, jnp.float32
 
     def up(r, c):
@@ -104,11 +109,11 @@
     def hb_copy(k, c):
         return remote(hb.at[0, tok(k)], hb.at[c, tok(k)], HB, step_sem.at[5, k], up(0, c))
 
-    share_sizes = (small, pair - small)
-
-    def share_of(source, m):
-        start = source * pair + (small if m else 0)
-        return pl.ds(pl.multiple_of(start, math.gcd(pair, small)), share_sizes[m])
+    def share_of(source, late, m):
+        start = sum(sizes[0]) + (source - 1) * sum(sizes[1]) if late else 0
+        if m:
+            start = start + sizes[late][0]
+        return pl.ds(pl.multiple_of(start, 16) if late else start, sizes[late][m])
 
     def as_core(do):
         for m in range(mates):
@@ -117,58 +122,70 @@
             def _():
                 do(m)
 
-    def fetch_a(m, c):
-        return remote(
-            wf.at[0, pl.ds(0, share_sizes[m])], wa.at[c, share_of(plane, m)], FA, fetch_sem.at[0], down(0, c)
-        )
-
-    def fetch_b(m, r):
-        return remote(
-            wf.at[1, pl.ds(0, share_sizes[m])], wb.at[r, share_of(plane, m)], FB, fetch_sem.at[1], down(r, 0)
+    def as_self(do):
+        for late in range(2):
+            for m in range(mates):
+
+                @pl.when(jnp.logical_and(core == m, plane > 0 if late else plane == 0))
+                def _():
+                    do(late, m)
+
+    def fetch_a(late, m, c):
+        return remote(
+            wf.at[0, pl.ds(0, sizes[late][m])], wa.at[c, share_of(plane, late, m)], FA, fetch_sem.at[0], down(0, c)
+        )
+
+    def fetch_b(late, m, r):
+        return remote(
+            wf.at[1, pl.ds(0, sizes[late][m])], wb.at[r, share_of(plane, late, m)], FB, fetch_sem.at[1], down(r, 0)
         )
 
     sides = ((wa, rest_cols), (wb, rest_rows))
 
-    def pass_on(source, side, m, to_plane):
+    def pass_on(source, side, late, m, to_plane):
         ref, rest = sides[side]
-        region = ref.at[rest, share_of(source, m)]
+        region = ref.at[rest, share_of(source, late, m)]
         return pltpu.make_async_remote_copy(
             src_ref=region, dst_ref=region, send_sem=sent_sem.at[ZA + side], recv_sem=land_sem.at[source, side],
             device_id={"dp": to_plane * mates + core}, device_id_type=MESH,
         )
 
-    def to_mate(source, side, m):
+    def to_mate(source, side, late, m):
         ref, rest = sides[side]
-        region = ref.at[rest, share_of(source, m)]
+        region = ref.at[rest, share_of(source, late, m)]
         return pltpu.make_async_remote_copy(
             src_ref=region, dst_ref=region, send_sem=sent_sem.at[MA + side], recv_sem=mate_sem.at[side],
             device_id={"dp": plane * mates + (mates - 1 - core)}, device_id_type=MESH,
         )
 
-    def spread(source, side, m, upward, downward):
+    def spread(source, side, late, m, upward, downward):
         if upward:
-            pl.when(plane + 1 < planes)(lambda: pass_on(source, side, m, plane + 1).start())
+            pl.when(plane + 1 < planes)(lambda: pass_on(source, side, late, m, plane + 1).start())
         if downward:
-            pl.when(plane > 0)(lambda: pass_on(source, side, m, plane - 1).start())
-        to_mate(source, side, m).start()
+            pl.when(plane > 0)(lambda: pass_on(source, side, late, m, plane - 1).start())
+        to_mate(source, side, late, m).start()
 
     def hop(h):
         below, above = plane - h, plane + h
 
         def relay(m):
             for side in range(2):
-
-                @pl.when(below >= 0)
-                def _():
-                    pass_on(below, side, m, plane).wait_recv()
-                    spread(below, side, m, True, False)
+                for late in range(2):
+
+                    @pl.when(below > 0 if late else below == 0)
+                    def _():
+                        pass_on(below, side, late, m, plane).wait_recv()
+                        spread(below, side, late, m, True, False)
 
                 @pl.when(above < planes)
                 def _():
-                    pass_on(above, side, m, plane).wait_recv()
-                    spread(above, side, m, False, True)
+                    pass_on(above, side, 1, m, plane).wait_recv()
+                    spread(above, side, 1, m, False, True)
 
         as_core(relay)
+
+    def rows_of(m):
+        return sizes[0][m] + (planes - 1) * sizes[1][m]
 
     def last_hops():
         def more(h, _):
@@ -180,7 +197,7 @@
     def landed():
         def from_mate(m):
             for side, (ref, rest) in enumerate(sides):
-                all_here(mate_sem.at[side], ref.at[rest, pl.ds(0, planes * share_sizes[1 - m])])
+                all_here(mate_sem.at[side], ref.at[rest, pl.ds(0, rows_of(1 - m))])
 
         as_core(from_mate)
 
@@ -217,11 +234,11 @@
             OB, out_sem.at[1], down(0, c),
         )
 
-    def load_share(m):
+    def load_share(late, m):
         return [
             pltpu.make_async_copy(
-                wd_ref.at[share_of(plane, m), pl.ds(side * side_cols, side_cols)],
-                wf.at[side, pl.ds(0, share_sizes[m])], load_sem.at[side],
+                wd_ref.at[share_of(plane, late, m), pl.ds(side * side_cols, side_cols)],
+                wf.at[side, pl.ds(0, sizes[late][m])], load_sem.at[side],
             )
             for side in range(2)
         ]
@@ -240,7 +257,7 @@
         pltpu.make_async_copy(wd_ref.at[:, pl.ds(side_cols, side_cols)], wb.at[0], load_sem.at[6 + chunks]),
     ]
 
-    as_core(lambda m: [load.start() for load in load_share(m)])
+    as_self(lambda late, m: [load.start() for load in load_share(late, m)])
     load_tokens.start()
 
     barrier = pltpu.get_barrier_semaphore()
@@ -255,16 +272,16 @@
     pl.when(plane + 1 < planes)(lambda: greet(group + mates))
     greet(plane * mates + (mates - 1 - core))
     neighbours = (plane > 0).astype(jnp.int32) + (plane + 1 < planes).astype(jnp.int32)
-    as_core(lambda m: [load.wait() for load in load_share(m)])
+    as_self(lambda late, m: [load.wait() for load in load_share(late, m)])
     pl.semaphore_wait(barrier, n - 1 + mates - 1 + neighbours)
 
-    def send_share(m):
+    def send_share(late, m):
         for c in range(1, cols):
-            fetch_a(m, c).start()
+            fetch_a(late, m, c).start()
         for r in range(1, rows):
-            fetch_b(m, r).start()
-
-    as_core(send_share)
+            fetch_b(late, m, r).start()
+
+    as_self(send_share)
     load_tokens.wait()
     for k in range(chunks):
         for r, c in by_reach:
@@ -273,12 +290,12 @@
         load.start()
 
     def fetch():
-        def take(m):
+        def take(late, m):
             for side, (ref, rest) in enumerate(sides):
-                all_here(fetch_sem.at[side], ref.at[rest, share_of(plane, m)])
-                spread(plane, side, m, True, True)
-
-        as_core(take)
+                all_here(fetch_sem.at[side], ref.at[rest, share_of(plane, late, m)])
+                spread(plane, side, late, m, True, True)
+
+        as_self(take)
         for load in loads:
             load.wait()
 
@@ -444,17 +461,23 @@
     all_sent(HA, ha.at[rest_rows])
     all_sent(HB, hb.at[rest_cols])
 
-    def shares_sent(m):
-        size = share_sizes[m]
+    def shares_sent(late, m):
         for side, (ref, rest) in enumerate(sides):
-            all_sent(FA + side, ref.at[rest, pl.ds(0, size)])
-            all_sent(MA + side, ref.at[rest, pl.ds(0, planes * size)])
-            if planes > 1:
-                inner = jnp.logical_and(plane > 0, plane + 1 < planes)
-                pl.when(inner)(lambda: all_sent(ZA + side, ref.at[rest, pl.ds(0, (planes + 1) * size)]))
-                pl.when(jnp.logical_not(inner))(lambda: all_sent(ZA + side, ref.at[rest, pl.ds(0, size)]))
-
-    as_core(shares_sent)
+
+            def drained(kind, size):
+                all_sent(kind + side, ref.at[rest, pl.ds(0, size)])
+
+            drained(FA, sizes[late][m])
+            drained(MA, rows_of(m))
+            if not late:
+                if planes > 1:
+                    drained(ZA, sizes[0][m])
+                continue
+            inner = plane + 1 < planes
+            pl.when(inner)(lambda: drained(ZA, rows_of(m) + sizes[1][m]))
+            pl.when(jnp.logical_not(inner))(lambda: drained(ZA, sizes[1][m]))
+
+    as_self(shares_sent)
     all_sent(OA, oa)
     all_sent(OB, ob)
     all_here(out_sem.at[0], oa)
@@ -470,7 +493,7 @@
         count, width = tokens.shape
         features, hidden = w_gate.shape
         side_cols = w_down.shape[1] // 2
-        pair = 2 * hidden // groups
+        largest = max(map(max, share_table(hidden, planes)))
         chunks = CHUNKS
         t = count // chunks
         bf16 = jnp.bfloat16
@@ -484,7 +507,7 @@
             out_specs=pl.BlockSpec(memory_space=pltpu.VMEM),
             scratch_shapes=[
                 pltpu.VMEM((count, width), bf16),
-                pltpu.VMEM((2, pair - small_share(pair), side_cols), bf16),
+                pltpu.VMEM((2, largest, side_cols), bf16),
                 pltpu.VMEM((features, hidden), bf16),
                 pltpu.VMEM((features, hidden), bf16),
                 pltpu.VMEM((cols, hidden, side_cols), bf16),

time: 68.2 us -> 67.8 us (level)
  Pallas kernels: 66.6 us -> 65.9 us
    pallas_call x1, Pallas kernels: 66.6 us -> 65.9 us  [shards(): pl.pallas_call(functools.partial(kernel, groups, rows, cols, chunks), out...]
where the time goes in v5:
time: 67.8 us; the launch traced here: 67.2 us
  Pallas kernels  65.9 us (97%)
  local copies, waits for them, and re-layouts  1.32 us (2%)
    pallas_call x1, Pallas kernels, shards(): pl.pallas_call(functools.partial(kernel, groups, rows, cols, chunks), out...  65.9 us

profile of v5, /device:TPU:0, one launch (start us, length us, event | category | flops | bytes accessed | tf_op | source)
XLA Modules:
  0.0 67.2 jit_solution(2279714088236761414)
XLA Ops:
  0.0 65.9 %shard_map.46 = bf16[128,8192]{1,0:T(8,128)(2,1)S(1)} custom-call(bf16[128,8192]{1,0:T(8,128)(2,1)} %x_ref.1, bf16[2048,1024]{1,0:T(8,128)(2,1)} %wg_ref.1, bf16[2048,1024]{1,0:T(8,128)(2,1)} %wu_ref.1, bf16[1024,2048]{1,0:T(8,128)(2,1)} %wd_ref.1), custom_call_target="tpu_custom_call" | custom-call | tf_op jit(solution)/shard_map/pallas_call | solution.py:503
  65.9 1.3 %copy.6 = bf16[128,8192]{1,0:T(8,128)(2,1)} copy(bf16[128,8192]{1,0:T(8,128)(2,1)S(1)} %shard_map.46) | data formatting | bytes 4194304

commit v6 on v5

--- a/solution.py
+++ b/solution.py
@@ -17,7 +17,7 @@
     "combine 2", "combine 3", "activate 0", "activate 1", "activate 2", "activate 3", "emit 0", "emit 1",
     "last hops", "local", "emit 2", "emit 3", "landed", "emit fetched",
 )
-X, A, B, C, D, HA, HB, OA, OB, FA, FB, ZA, ZB, MA, MB = range(15)
+X, AB, CD, H, OA, OB, FA, FB, ZA, ZB, MA, MB = range(12)
 
 
 def tile_of(width, most):
@@ -40,7 +40,7 @@
 def kernel(
     groups, rows, cols, chunks,
     x_ref, wg_ref, wu_ref, wd_ref, out_ref,
-    xin, wf, wg, wu, wa, wb, xbuf, acc, part, rec_a, rec_b, sum_a, sum_b, fin_a, fin_b, ha, hb, oa, ob,
+    xin, wf, wg, wu, wa, wb, xbuf, acc, part, rec, sum_a, sum_b, fin, held, oa, ob,
     load_sem, sent_sem, x_sem, step_sem, fetch_sem, land_sem, mate_sem, out_sem,
 ):
     n = rows * cols
@@ -91,23 +91,34 @@
             xin.at[tok(k), shard(to, features)], xbuf.at[k, pl.ds((r * cols + c) * t, t)], X, x_sem.at[k], to
         )
 
+    from_b = (rows - 1) * cols
+
+    def at_a(r, c):
+        return (r - 1) * cols + c
+
+    def at_b(c, r):
+        return from_b + (c - 1) * rows + r
+
     def a_copy(k, r):
-        return remote(part.at[k, 0, r], rec_a.at[k, r], A, step_sem.at[0, k], down(r, 0))
+        return remote(part.at[k, 0, r], rec.at[k, pl.ds(at_a(r, 0), cols)], AB, step_sem.at[0, k], down(r, 0))
 
     def b_copy(k, c):
-        return remote(part.at[k, 1, :, c], rec_b.at[k, c], B, step_sem.at[1, k], down(0, c))
+        return remote(part.at[k, 1, :, c], rec.at[k, pl.ds(at_b(c, 0), rows)], AB, step_sem.at[0, k], down(0, c))
 
     def c_copy(k, c):
-        return remote(sum_a.at[k, c], fin_a.at[k, c], C, step_sem.at[2, k], down(0, c))
+        return remote(sum_a.at[k, c], fin.at[k, c - 1], CD, step_sem.at[1, k], down(0, c))
 
     def d_copy(k, r):
-        return remote(sum_b.at[k, r], fin_b.at[k, r], D, step_sem.at[3, k], down(r, 0))
+        return remote(sum_b.at[k, r], fin.at[k, cols - 2 + r], CD, step_sem.at[1, k], down(r, 0))
+
+    mine = rows - 1
+    from_rows, from_cols = pl.ds(0, rows - 1), pl.ds(rows, cols - 1)
 
     def ha_copy(k, r):
-        return remote(ha.at[0, tok(k)], ha.at[r, tok(k)], HA, step_sem.at[4, k], up(r, 0))
+        return remote(held.at[mine, tok(k)], held.at[r - 1, tok(k)], H, step_sem.at[2, k], up(r, 0))
 
     def hb_copy(k, c):
-        return remote(hb.at[0, tok(k)], hb.at[c, tok(k)], HB, step_sem.at[5, k], up(0, c))
+        return remote(held.at[mine, tok(k)], held.at[mine + c, tok(k)], H, step_sem.at[2, k], up(0, c))
 
     def share_of(source, late, m):
         start = sum(sizes[0]) + (source - 1) * sum(sizes[1]) if late else 0
@@ -272,12 +283,14 @@
     pl.when(plane + 1 < planes)(lambda: greet(group + mates))
     greet(plane * mates + (mates - 1 - core))
     neighbours = (plane > 0).astype(jnp.int32) + (plane + 1 < planes).astype(jnp.int32)
-    as_self(lambda late, m: [load.wait() for load in load_share(late, m)])
     pl.semaphore_wait(barrier, n - 1 + mates - 1 + neighbours)
 
     def send_share(late, m):
+        share_a, share_b = load_share(late, m)
+        share_a.wait()
         for c in range(1, cols):
             fetch_a(late, m, c).start()
+        share_b.wait()
         for r in range(1, rows):
             fetch_b(late, m, r).start()
 
@@ -325,40 +338,37 @@
             b_copy(k, c).start()
 
     def combine(k):
-        all_here(step_sem.at[0, k], rec_a.at[k, rest_rows])
+        all_here(step_sem.at[0, k], rec.at[k])
         for c in range(1, cols):
             total = part[k, 0, 0, c].astype(f32)
             for r in range(1, rows):
-                total = total + rec_a[k, r, c].astype(f32)
+                total = total + rec[k, at_a(r, c)].astype(f32)
             sum_a[k, c] = total.astype(bf16)
             c_copy(k, c).start()
-        all_here(step_sem.at[1, k], rec_b.at[k, rest_cols])
         for r in range(1, rows):
             total = part[k, 1, r, 0].astype(f32)
             for c in range(1, cols):
-                total = total + rec_b[k, c, r].astype(f32)
+                total = total + rec[k, at_b(c, r)].astype(f32)
             sum_b[k, r] = total.astype(bf16)
             d_copy(k, r).start()
 
     def activate(k):
-        all_here(step_sem.at[2, k], fin_a.at[k, rest_cols])
-        all_here(step_sem.at[3, k], fin_b.at[k, rest_rows])
+        all_here(step_sem.at[1, k], fin.at[k])
         for side in range(2):
             total = acc[k, side]
             if side == 0:
                 for r in range(1, rows):
-                    total = total + rec_a[k, r, 0].astype(f32)
+                    total = total + rec[k, at_a(r, 0)].astype(f32)
                 for c in range(1, cols):
-                    total = total + fin_a[k, c].astype(f32)
+                    total = total + fin[k, c - 1].astype(f32)
             else:
                 for c in range(1, cols):
-                    total = total + rec_b[k, c, 0].astype(f32)
+                    total = total + rec[k, at_b(c, 0)].astype(f32)
                 for r in range(1, rows):
-                    total = total + fin_b[k, r].astype(f32)
+                    total = total + fin[k, cols - 2 + r].astype(f32)
             gate = total[:, :half]
             done = (gate / (1.0 + jnp.exp(-gate)) * total[:, half:]).astype(bf16)
-            ha[0, tok(k), pl.ds(side * half, half)] = done
-            hb[0, tok(k), pl.ds(side * half, half)] = done
+            held[mine, tok(k), pl.ds(side * half, half)] = done
         for r in range(1, rows):
             ha_copy(k, r).start()
         for c in range(1, cols):
@@ -368,16 +378,15 @@
     wides = side_cols // wide
 
     def emit(k):
-        all_here(step_sem.at[4, k], ha.at[rest_rows, tok(k)])
-        theirs = ha[rest_rows, tok(k)].reshape((rows - 1) * t, hidden)
+        all_here(step_sem.at[2, k], held.at[pl.ds(0, rows + cols - 2), tok(k)])
+        theirs = held[from_rows, tok(k)].reshape((rows - 1) * t, hidden)
         for j in range(wides):
             where = pl.ds(j * wide, wide)
             got = jnp.dot(theirs, wa[0, :, where], preferred_element_type=f32).astype(bf16)
             oa[0, :, tok(k), where] = got.reshape(rows - 1, t, wide)
         for r in range(1, rows):
             oa_copy(k, r).start()
-        all_here(step_sem.at[5, k], hb.at[rest_cols, tok(k)])
-        theirs = hb[rest_cols, tok(k)].reshape((cols - 1) * t, hidden)
+        theirs = held[from_cols, tok(k)].reshape((cols - 1) * t, hidden)
         for j in range(wides):
             where = pl.ds(j * wide, wide)
             got = jnp.dot(theirs, wb[0, :, where], preferred_element_type=f32).astype(bf16)
@@ -390,7 +399,7 @@
             where = pl.ds(pl.multiple_of(j * wide, wide), wide)
             for side, w in ((0, wa), (1, wb)):
                 out_ref[:, columns((row, col), side, j * wide, wide)] = jnp.dot(
-                    ha[0], w[0, :, where], preferred_element_type=f32
+                    held[mine], w[0, :, where], preferred_element_type=f32
                 ).astype(bf16)
             return 0
 
@@ -400,10 +409,10 @@
         c, j = 1 + i // out_tiles, lax.rem(i, out_tiles)
         where = pl.ds(pl.multiple_of(j * out_tile, out_tile), out_tile)
         got = jnp.dot(
-            ha[...].reshape(rows * count, hidden), wa[c, :, where], preferred_element_type=f32
+            held[pl.ds(0, rows)].reshape(rows * count, hidden), wa[c, :, where], preferred_element_type=f32
         ).astype(bf16)
-        oa[c, :, :, where] = got[count:].reshape(rows - 1, count, out_tile)
-        out_ref[:, columns(up(0, c), 0, j * out_tile, out_tile)] = got[:count]
+        oa[c, :, :, where] = got[: mine * count].reshape(rows - 1, count, out_tile)
+        out_ref[:, columns(up(0, c), 0, j * out_tile, out_tile)] = got[mine * count :]
         for r in range(1, rows):
             ga_copy(c, j, r).start()
 
@@ -411,7 +420,7 @@
         r, j = 1 + i // out_tiles, lax.rem(i, out_tiles)
         where = pl.ds(pl.multiple_of(j * out_tile, out_tile), out_tile)
         got = jnp.dot(
-            hb[...].reshape(cols * count, hidden), wb[r, :, where], preferred_element_type=f32
+            held[pl.ds(mine, cols)].reshape(cols * count, hidden), wb[r, :, where], preferred_element_type=f32
         ).astype(bf16)
         ob[r, :, :, where] = got[count:].reshape(cols - 1, count, out_tile)
         out_ref[:, columns(up(r, 0), 1, j * out_tile, out_tile)] = got[:count]
@@ -454,12 +463,9 @@
                 stages[name](int(at))
 
     all_sent(X, xbuf.at[:, pl.ds(t, (n - 1) * t)])
-    all_sent(A, rec_a.at[:, rest_rows])
-    all_sent(B, rec_b.at[:, rest_cols])
-    all_sent(C, fin_a.at[:, rest_cols])
-    all_sent(D, fin_b.at[:, rest_rows])
-    all_sent(HA, ha.at[rest_rows])
-    all_sent(HB, hb.at[rest_cols])
+    all_sent(AB, rec)
+    all_sent(CD, fin)
+    all_sent(H, held.at[pl.ds(0, rows + cols - 2)])
 
     def shares_sent(late, m):
         for side, (ref, rest) in enumerate(sides):
@@ -515,20 +521,17 @@
                 pltpu.VMEM((chunks, n * t, features), bf16),
                 pltpu.VMEM((chunks, 2, t, hidden), jnp.float32),
                 pltpu.VMEM((chunks, 2, rows, cols, t, hidden), bf16),
-                pltpu.VMEM((chunks, rows, cols, t, hidden), bf16),
-                pltpu.VMEM((chunks, cols, rows, t, hidden), bf16),
+                pltpu.VMEM((chunks, (rows - 1) * cols + (cols - 1) * rows, t, hidden), bf16),
                 pltpu.VMEM((chunks, cols, t, hidden), bf16),
                 pltpu.VMEM((chunks, rows, t, hidden), bf16),
-                pltpu.VMEM((chunks, cols, t, hidden), bf16),
-                pltpu.VMEM((chunks, rows, t, hidden), bf16),
-                pltpu.VMEM((rows, count, hidden), bf16),
-                pltpu.VMEM((cols, count, hidden), bf16),
+                pltpu.VMEM((chunks, rows + cols - 2, t, hidden), bf16),
+                pltpu.VMEM((rows + cols - 1, count, hidden), bf16),
                 pltpu.VMEM((cols, rows - 1, count, side_cols), bf16),
                 pltpu.VMEM((rows, cols - 1, count, side_cols), bf16),
                 dma((7 + chunks,)),
-                dma((15,)),
+                dma((12,)),
                 dma((chunks,)),
-                dma((6, chunks)),
+                dma((3, chunks)),
                 dma((2,)),
                 dma((planes, 2)),
                 dma((2,)),

time: 67.8 us -> 67.6 us (level)
  no operation moved by 1% of the time
where the time goes in v6:
time: 67.6 us; the launch traced here: 67.1 us
  Pallas kernels  65.7 us (97%)
  local copies, waits for them, and re-layouts  1.32 us (2%)
    pallas_call x1, Pallas kernels, shards(): pl.pallas_call(functools.partial(kernel, groups, rows, cols, chunks), out...  65.7 us

profile of v6, /device:TPU:0, one launch (start us, length us, event | category | flops | bytes accessed | tf_op | source)
XLA Modules:
  0.0 67.1 jit_solution(14721003459651360650)
XLA Ops:
  0.0 65.7 %shard_map.46 = bf16[128,8192]{1,0:T(8,128)(2,1)S(1)} custom-call(bf16[128,8192]{1,0:T(8,128)(2,1)} %x_ref.1, bf16[2048,1024]{1,0:T(8,128)(2,1)} %wg_ref.1, bf16[2048,1024]{1,0:T(8,128)(2,1)} %wu_ref.1, bf16[1024,2048]{1,0:T(8,128)(2,1)} %wd_ref.1), custom_call_target="tpu_custom_call" | custom-call | tf_op jit(solution)/shard_map/pallas_call | solution.py:509
  65.7 1.3 %copy.6 = bf16[128,8192]{1,0:T(8,128)(2,1)} copy(bf16[128,8192]{1,0:T(8,128)(2,1)S(1)} %shard_map.46) | data formatting | bytes 4194304
